TPU v7x, 32 devices: a whole 2x2x4 slice. The times are simulated.
32 devices in a mesh: tm: 8 (over z, y), col: 4 (over x, core).
Axes of the slice: x: 2, y: 2, z: 4, core: 2. Of those that a mesh axis runs over, the one named last changes fastest.
Arguments:
- block_values: bfloat16 [4, 16384, 128], P('col', 'tm'), may hold values from -6 to 6
- block_shifts: bfloat16 [4, 16384, 128], P('col', 'tm'), may hold values from -1 to 1
- block_sensor: int32 [4, 16384], P('col', 'tm'), may hold values from 0 to 4095
- block_window: int32 [4, 16384], P('col', 'tm'), may hold values from 0 to 3
- block_owner: int32 [4, 16384, 1], P('col', 'tm'), may hold values from 0 to 7; in each aligned block of 2048 rows (0 to 2047, 2048 to 4095, ..., all dimensions but the last counted through in order) at most 384 rows name the same one
- block_counts: int32 [4, 8], P('col', 'tm'), may hold values from 1536 to 2048
- calibration: bfloat16 [16384, 4096], P('tm', 'col'), may hold values from -0.046875 to 0.046875
Outputs:
- calibrated: bfloat16 [4096, 4096], P('tm', 'col')
Inputs may be any that keep to these rules, and one draw needn't show every extreme that they name: `block_owner`: among the 2048 block slots of one device, at most 384 name the same owner, a bound that some block reaches. The live blocks of device (tm t, col c) are its first block_counts[c, t] slots.
All inputs are finite; a program needn't handle non-finite values.
Results may differ from a plain program's by a relative error of at most 0.015.
Values may be sent and summed in bfloat16 or wider, within the bound.
No kernel may reach another device: no remote copies, remote signals or barrier semaphores. Data moves between devices by JAX's collectives and lax.ppermute only.
A program may use at most 128 MiB of HBM per device.

v0:
```python
import jax
import jax.numpy as jnp
from jax import lax
from jax.sharding import PartitionSpec as P

SENSORS = 16384
ROWS_DEV = 512


def spread_samples(values, shifts):
    samples = values.astype(jnp.float32)
    offsets = shifts.astype(jnp.float32)
    result = jnp.zeros(samples.shape, jnp.float32)
    lead = [(0, 0)] * (samples.ndim - 1)
    for displace in (-1, 0, 1):
        weight = jnp.maximum(0.0, 1.0 - jnp.abs(offsets - displace)).astype(jnp.bfloat16)
        weight = lax.optimization_barrier(weight).astype(jnp.float32)
        product = weight * samples
        if displace == 1:
            result = result + jnp.pad(product[..., :-1], lead + [(1, 0)])
        elif displace == -1:
            result = jnp.pad(product[..., 1:], lead + [(0, 1)])
        else:
            result = result + product
    return result


def spread_slots(moved_slots):
    return spread_samples(moved_slots[:, :, 0], moved_slots[:, :, 1])


def per_device(
    block_values, block_shifts, block_sensor, block_window, block_owner, block_counts, calibration
):
    values = block_values[0]
    shifts = block_shifts[0]
    blocks = values.shape[0]
    length = values.shape[1]
    owners = lax.axis_size("tm")
    group_size = SENSORS // lax.axis_size("col")
    windows = ROWS_DEV // length
    capacity = blocks * 3 // (2 * owners)
    slot_total = owners * capacity
    block_index = lax.iota(jnp.int32, blocks)
    is_live = block_index < block_counts[0, 0]
    values = jnp.where(is_live[:, None], values, jnp.zeros_like(values))
    owner_ids = block_owner[0, :, 0]
    owner_onehot = (owner_ids[:, None] == lax.iota(jnp.int32, owners)[None, :]).astype(jnp.bfloat16)
    lower_mask = (block_index[:, None] > block_index[None, :]).astype(jnp.bfloat16)
    earlier = jnp.dot(lower_mask, owner_onehot, preferred_element_type=jnp.float32)
    slot_rank = jnp.sum(earlier * owner_onehot.astype(jnp.float32), axis=1).astype(jnp.int32)
    slot_index = owner_ids * capacity + slot_rank
    slot_match = slot_index[None, :] == lax.iota(jnp.int32, slot_total)[:, None]
    source = jnp.max(jnp.where(slot_match, block_index[None, :], -1), axis=1)
    filled = source >= 0
    source_row = jnp.maximum(source, 0)
    row_keys = block_window[0] * group_size + block_sensor[0]
    payload = jnp.stack((values, shifts), axis=1)
    outgoing = jnp.where(
        filled[:, None, None], jnp.take(payload, source_row, axis=0), jnp.zeros((), jnp.bfloat16)
    )
    outgoing = outgoing.reshape(owners, capacity, 2, length)
    outgoing_keys = jnp.where(filled, jnp.take(row_keys, source_row, axis=0), 0).reshape(
        owners, capacity
    )
    contribution = spread_slots(
        lax.all_to_all(outgoing, "tm", split_axis=0, concat_axis=0, tiled=True)
    )
    incoming_keys = lax.all_to_all(outgoing_keys, "tm", split_axis=0, concat_axis=0, tiled=True)
    flat_keys = incoming_keys.reshape(-1)
    flat_contrib = contribution.reshape(-1, length)
    upper_part = flat_contrib.astype(jnp.bfloat16)
    lower_part = (flat_contrib - upper_part.astype(jnp.float32)).astype(jnp.bfloat16)
    sensor_iota = lax.iota(jnp.int32, group_size)
    window_rows = []
    for window in range(windows):
        target = flat_keys - window * group_size
        place_onehot = (target[:, None] == sensor_iota[None, :]).astype(jnp.bfloat16)
        dims = (((0,), (0,)), ((), ()))
        window_sum = lax.dot_general(
            upper_part, place_onehot, dims, preferred_element_type=jnp.float32
        )
        window_sum = window_sum + lax.dot_general(
            lower_part, place_onehot, dims, preferred_element_type=jnp.float32
        )
        window_rows.append(window_sum)
    aligned = jnp.concatenate(window_rows, axis=0).astype(jnp.bfloat16)
    gathered = lax.all_gather(aligned, "col", axis=1, tiled=True)
    regrouped = lax.all_to_all(gathered, "tm", split_axis=1, concat_axis=0, tiled=True)
    return lax.psum_scatter(
        jnp.dot(regrouped, calibration, preferred_element_type=jnp.float32).astype(jnp.bfloat16),
        "tm",
        scatter_dimension=0,
        tiled=True,
    )


def solution(mesh):
    placed = (
        P("col", "tm", None),
        P("col", "tm", None),
        P("col", "tm"),
        P("col", "tm"),
        P("col", "tm", None),
        P("col", "tm"),
        P("tm", "col"),
    )
    return jax.shard_map(
        per_device, mesh=mesh, in_specs=placed, out_specs=P("tm", "col"), check_vma=False
    )
```

profile of v0, /device:TPU:0, one launch (start us, length us, event | category | flops | bytes accessed | tf_op | source)
XLA Modules:
  0.0 889.2 jit_solution(16694593911328433421)
XLA Ops:
  6.5 0.0 copy-start.4
  6.5 0.0 copy-start.5
  6.5 0.0 copy-start.6
  6.5 2.2 fusion.38
  8.8 0.0 copy-done.4
  8.8 3.4 select_reduce_fusion
  12.2 0.0 copy-done.5
  12.2 0.0 copy-done.6
  12.3 0.0 copy-start.2
  12.3 0.0 copy-start.3
  12.3 17.4 %gather_fusion.1 = s32[3072]{0:T(1024)S(1)} fusion(s32[2048]{0:T(1024)S(1)} %bitcast.39, s32[3072]{0:T(1024)S(1)} %maximum_clamp_fusion), kind=kCustom, calls=%fused_computation.1 | custom fusion | bytes 36864 | tf_op jit(solution)/shard_map/jit(_take)/gather | solution.py:63
  29.7 0.6 select_select_fusion
  30.3 7.5 all-to-all-start.1
  38.6 0.0 copy-done.2
  38.6 8.1 copy.15
  46.7 0.0 copy-done.3
  46.7 15.2 %broadcast_select_fusion.2 = bf16[2048,1,128]{2,1,0:T(2,128)(2,1)S(1)} fusion(pred[2048]{0:T(1024)(128)(4,1)S(1)} %iota_compare_fusion.37, bf16[2048,1,128]{2,0,1:T(8,128)(2,1)S(1)} %bitcast.47), kind=kLoop, calls=%fused_computation.43 | loop fusion | flops 262144 | bytes 1050624 | tf_op jit(solution)/shard_map/jit(_where)/select_n | solution.py:46
  61.9 2.4 pad_maximum_fusion.1
  64.4 10.4 %gather_fusion = bf16[3072,2,128]{2,1,0:T(2,128)(2,1)S(1)} fusion(bf16[2048,2,128]{2,1,0:T(2,128)(2,1)S(1)} %pad_maximum_fusion.1, s32[3072]{0:T(1024)S(1)} %maximum_clamp_fusion), kind=kCustom, calls=%fused_computation | custom fusion | bytes 3158016 | tf_op jit(solution)/shard_map/jit(_take)/gather | solution.py:60
  74.8 9.5 %broadcast_select_fusion.1 = bf16[8,384,2,128]{3,2,1,0:T(2,128)(2,1)} fusion(pred[8,384]{1,0:T(8,128)(4,1)S(1)} %ge.33, bf16[8,384,2,128]{3,2,1,0:T(2,128)(2,1)S(1)} %bitcast.45, pred[8,384]{1,0:T(8,128)(4,1)S(1)} %le.30), kind=kLoop, calls=%fused_computation.38 | loop fusion | flops 1572864 | bytes 3151872 | tf_op jit(solution)/shard_map/jit(_where)/select_n | solution.py:59
  84.2 0.0 all-to-all-done.1
  84.2 6.0 all-to-all-start
  90.2 0.0 all-gather.2.cloned.1.call-start
  90.3 36.4 %all-to-all-done = bf16[8,384,2,128]{3,2,1,0:T(2,128)(2,1)S(1)} async-done(((bf16[8,384,2,128]{3,2,1,0:T(2,128)(2,1)}), bf16[8,384,2,128]{3,2,1,0:T(2,128)(2,1)S(1)}, u32[]{:S(2)}, u32[]{:S(2)}) %all-to-all-start) | async-done | bytes 1572896 | tf_op jit(solution)/shard_map/all_to_all | solution.py:67
  126.7 2.6 fusion.44
  129.3 0.8 fusion.41
  130.1 0.7 slice_multiply_fusion.1
  130.9 0.6 pad_add_fusion
  131.4 0.2 fusion.37
  131.7 0.0 copy-start.1
  131.7 0.0 copy-start
  131.7 11.8 %fusion.6 = f32[128,4096]{1,0:T(8,128)} fusion(bf16[3072,128]{1,0:T(8,128)(2,1)S(1)} %get-tuple-element.8, s32[3072]{0:T(1024)S(1)} %bitcast.49), kind=kOutput, calls=%fused_computation.12 | convolution fusion | flops 3233808384 | bytes 2895872 | tf_op jit(solution)/shard_map/dot_general | solution.py:83
  143.5 11.9 %fusion = f32[128,4096]{1,0:T(8,128)} fusion(bf16[3072,128]{1,0:T(8,128)(2,1)S(1)} %get-tuple-element.8, s32[3072]{0:T(1024)S(1)} %get-tuple-element.18), kind=kOutput, calls=%fused_computation.3 | convolution fusion | flops 3233808384 | bytes 2895872 | tf_op jit(solution)/shard_map/dot_general | solution.py:83
  155.4 0.0 copy-done.1
  155.4 12.0 %fusion.2 = f32[128,4096]{1,0:T(8,128)} fusion(bf16[3072,128]{1,0:T(8,128)(2,1)S(1)} %get-tuple-element.8, s32[3072]{0:T(1024)S(1)} %get-tuple-element.19), kind=kOutput, calls=%fused_computation.6 | convolution fusion | flops 3233808384 | bytes 2895872 | tf_op jit(solution)/shard_map/dot_general | solution.py:83
  167.4 12.5 %fusion.21 = bf16[128,4096]{1,0:T(8,128)(2,1)S(1)} fusion(f32[128,4096]{1,0:T(8,128)} %fusion, bf16[3072,128]{1,0:T(8,128)(2,1)S(1)} %get-tuple-element.9, s32[3072]{0:T(1024)S(1)} %get-tuple-element.18), kind=kOutput, calls=%fused_computation.32 | convolution fusion | flops 3234856960 | bytes 3944448 | tf_op jit(solution)/shard_map/dot_general | solution.py:80
  180.0 0.0 copy-done
  180.0 12.3 %fusion.22 = bf16[128,4096]{1,0:T(8,128)(2,1)S(1)} fusion(f32[128,4096]{1,0:T(8,128)} %fusion.2, bf16[3072,128]{1,0:T(8,128)(2,1)S(1)} %get-tuple-element.9, s32[3072]{0:T(1024)S(1)} %get-tuple-element.19), kind=kOutput, calls=%fused_computation.33 | convolution fusion | flops 3234856960 | bytes 3944448 | tf_op jit(solution)/shard_map/dot_general | solution.py:80
  192.3 12.9 %fusion.4 = f32[128,4096]{1,0:T(8,128)} fusion(bf16[3072,128]{1,0:T(8,128)(2,1)} %copy-done.1, s32[3072]{0:T(1024)S(1)} %get-tuple-element.17), kind=kOutput, calls=%fused_computation.9 | convolution fusion | flops 3233808384 | bytes 2895872 | tf_op jit(solution)/shard_map/dot_general | solution.py:83
  205.2 12.6 %fusion.23 = bf16[128,4096]{1,0:T(8,128)(2,1)S(1)} fusion(f32[128,4096]{1,0:T(8,128)} %fusion.4, bf16[3072,128]{1,0:T(8,128)(2,1)} %copy-done, s32[3072]{0:T(1024)S(1)} %get-tuple-element.17), kind=kOutput, calls=%fused_computation.34 | convolution fusion | flops 3234856960 | bytes 3944448 | tf_op jit(solution)/shard_map/dot_general | solution.py:80
  217.8 13.6 %fusion.24 = bf16[128,4096]{1,0:T(8,128)(2,1)} fusion(f32[128,4096]{1,0:T(8,128)} %fusion.6, bf16[3072,128]{1,0:T(8,128)(2,1)} %copy-done, s32[3072]{0:T(1024)S(1)} %bitcast.50), kind=kOutput, calls=%fused_computation.35 | convolution fusion | flops 3234856960 | bytes 3944448 | tf_op jit(solution)/shard_map/dot_general | solution.py:80
  231.4 3.2 pad_maximum_fusion
  234.5 0.0 all-gather.2.cloned.1.call-update
  234.6 0.0 reduce-scatter.2.cloned.1.call-start
  234.6 105.1 %all-gather.2.cloned.1.call-done = bf16[512,16384]{1,0:T(8,128)(2,1)} async-done(((bf16[512,4096]{1,0:T(8,128)(2,1)}), bf16[512,16384]{1,0:T(8,128)(2,1)}) %all-gather.2.cloned.1.call-update) | async-done | bytes 16777232 | tf_op jit(solution)/shard_map/all_gather | solution.py:88
  339.7 8.0 copy.25
  347.7 0.0 copy-start.7
  347.7 368.8 %all_to_all.30 = bf16[512,8,2048]{2,0,1:T(8,128)(2,1)S(1)} all-to-all(bf16[512,8,2048]{2,0,1:T(8,128)(2,1)S(1)} %bitcast.40), channel_id=1, replica_groups=mesh['tm'=8,'col'=4] {'tm'}, dimensions={1} | all-to-all | bytes 33554432 | tf_op jit(solution)/shard_map/all_to_all | solution.py:89
  716.5 0.0 copy-done.7
  716.5 19.3 %convolution_convert_fusion = bf16[4096,1024]{1,0:T(8,128)(2,1)} fusion(bf16[4096,2048]{1,0:T(8,128)(2,1)S(1)} %bitcast.44, bf16[2048,1024]{1,0:T(8,128)(2,1)S(1)} %copy-done.7), kind=kOutput, calls=%fused_computation.27 | convolution fusion | flops 17184063488 | bytes 29360128 | tf_op jit(solution)/shard_map/dot_general | solution.py:91
  735.8 0.0 reduce-scatter.2.cloned.1.call-update
  735.8 146.2 %reduce-scatter.2.cloned.1.call-done = bf16[512,1024]{1,0:T(8,128)(2,1)} async-done(((bf16[4096,1024]{1,0:T(8,128)(2,1)}), bf16[512,1024]{1,0:T(8,128)(2,1)}) %reduce-scatter.2.cloned.1.call-update) | async-done | bytes 1048592 | tf_op jit(solution)/shard_map/reduce_scatter | solution.py:90
  (7 shorter events, 0.1 us)
Async XLA Ops:
  6.5 2.2 copy-start.4
  6.5 5.7 copy-start.5
  6.5 5.7 copy-start.6
  12.3 26.3 %copy-start.2 = (bf16[1,2048,128]{2,1,0:T(8,128)(2,1)S(1)}, bf16[1,2048,128]{2,1,0:T(8,128)(2,1)}, u32[]{:S(2)}) copy-start(bf16[1,2048,128]{2,1,0:T(8,128)(2,1)} %param.8) | copy-start | bytes 1572868
  12.3 34.5 %copy-start.3 = (bf16[1,2048,128]{2,1,0:T(8,128)(2,1)S(1)}, bf16[1,2048,128]{2,1,0:T(8,128)(2,1)}, u32[]{:S(2)}) copy-start(bf16[1,2048,128]{2,1,0:T(8,128)(2,1)} %param.7) | copy-start | bytes 1572868
  30.3 53.9 %all-to-all-start.1 = ((s32[8,1,384]{2,1,0:T(1,128)}), s32[8,1,384]{2,1,0:T(1,128)S(1)}, u32[]{:S(2)}, u32[]{:S(2)}) async-start(s32[8,1,384]{2,1,0:T(1,128)} %bitcast.11), calls=%async_computation.1 | async-start | bytes 24576 | tf_op jit(solution)/shard_map/all_to_all | solution.py:69
  84.2 42.4 %all-to-all-start = ((bf16[8,384,2,128]{3,2,1,0:T(2,128)(2,1)}), bf16[8,384,2,128]{3,2,1,0:T(2,128)(2,1)S(1)}, u32[]{:S(2)}, u32[]{:S(2)}) async-start(bf16[8,384,2,128]{3,2,1,0:T(2,128)(2,1)} %broadcast_select_fusion.1), calls=%async_computation | async-start | bytes 3145728 | tf_op jit(solution)/shard_map/all_to_all | solution.py:67
  90.2 249.4 %all-gather.2.cloned.1.call-start = ((), (), s32[]{:S(2)}) async-start(), calls=%async_computation.4 | async-start | bytes 20971520 | tf_op jit(solution)/shard_map/all_gather | solution.py:88
  131.7 23.8 %copy-start.1 = (bf16[3072,128]{1,0:T(8,128)(2,1)}, bf16[3072,128]{1,0:T(8,128)(2,1)S(1)}, u32[]{:S(2)}) copy-start(bf16[3072,128]{1,0:T(8,128)(2,1)S(1)} %get-tuple-element.8) | copy-start | bytes 2359300
  131.7 48.3 %copy-start = (bf16[3072,128]{1,0:T(8,128)(2,1)}, bf16[3072,128]{1,0:T(8,128)(2,1)S(1)}, u32[]{:S(2)}) copy-start(bf16[3072,128]{1,0:T(8,128)(2,1)S(1)} %get-tuple-element.9) | copy-start | bytes 2359300
  234.6 647.4 %reduce-scatter.2.cloned.1.call-start = ((), (), s32[]{:S(2)}) async-start(), calls=%async_computation.5 | async-start | bytes 9437184 | tf_op jit(solution)/shard_map/reduce_scatter | solution.py:90
  347.7 368.8 %copy-start.7 = (bf16[2048,1024]{1,0:T(8,128)(2,1)S(1)}, bf16[2048,1024]{1,0:T(8,128)(2,1)}, u32[]{:S(2)}) copy-start(bf16[2048,1024]{1,0:T(8,128)(2,1)} %param.13) | copy-start | bytes 12582916
Sparse Core Ops, SparseCore 0:
  234.7 104.9 all-gather.1
  735.9 145.9 reduce-scatter.1
where the time goes:
time: 894 us; the launch traced here: 889 us
  blocking collectives  369 us (41%)
  waiting for transfers between devices  288 us (32%)
  matrix products  121 us (14%)
  local copies, waits for them, and re-layouts  44 us (5%)
  other arithmetic  39.2 us (4%)
  between operations  14.7 us (2%)
  starting transfers between devices  13.6 us (2%)
    all_to_all x1, blocking collectives, per_device(): lax.all_to_all(gathered, 'tm', split_axis=1, concat_axis=0, tiled=True)  369 us
    reduce_scatter x1, waiting for transfers between devices, per_device(): lax.psum_scatter(jnp.dot(regrouped, calibration, preferred_element_type=j...  146 us
    all_gather x1, waiting for transfers between devices, per_device(): gathered = lax.all_gather(aligned, 'col', axis=1, tiled=True)  105 us
    dot_general x4, matrix products, per_device(): lax.dot_general(upper_part, place_onehot, dims, preferred_element_type=jn...  51 us
    dot_general x4, matrix products, per_device(): lax.dot_general(lower_part, place_onehot, dims, preferred_element_type=jn...  48.6 us
    all_to_all x1, waiting for transfers between devices, per_device(): lax.all_to_all(outgoing, 'tm', split_axis=0, concat_axis=0, tiled=True)  36.4 us
    dot_general x1, matrix products, per_device(): jnp.dot(regrouped, calibration, preferred_element_type=jnp.float32)  19.3 us
  transfers between devices with their start and end apart: 4, of which 3 were waited for; matrix products, arithmetic and copies ran while one was open for 5% of the time, Pallas kernels for 0%

commit v1 on v0

v1 whole, which is shorter than its diff:
```python
import functools

import jax
import jax.numpy as jnp
from jax import lax
from jax.experimental import pallas as pl
from jax.experimental.pallas import tpu as pltpu
from jax.sharding import Mesh, PartitionSpec as P

ROWS_DEV = 512
GROUP = 16
KEY_ROWS = 16


def spread_kernel(count_ref, values_ref, shifts_ref, keys_ref, digits_ref, out_ref):
    chunk, length = values_ref.shape
    row = lax.broadcasted_iota(jnp.int32, (length, length), 0)
    lane = lax.broadcasted_iota(jnp.int32, (length, length), 1)
    same_group = (row // GROUP == lane // GROUP) & (lane <= row)
    first = pl.program_id(0) * chunk
    for tile in range(chunk // length):
        at = pl.ds(tile * length, length)
        samples = values_ref[at, :].astype(jnp.float32)
        offsets = shifts_ref[at, :].astype(jnp.float32)

        def weighted(displace):
            weight = jnp.maximum(0.0, 1.0 - jnp.abs(offsets - displace))
            return weight.astype(jnp.bfloat16).astype(jnp.float32) * samples

        before = jnp.where(lane == length - 1, 0.0, pltpu.roll(weighted(-1.0), length - 1, 1))
        after = jnp.where(lane == 0, 0.0, pltpu.roll(weighted(1.0), 1, 1))
        total = before + weighted(0.0) + after
        live = row + (first + tile * length) < count_ref[0, 0]
        total = jnp.where(live, total, 0.0).astype(jnp.bfloat16)
        across = jnp.broadcast_to(keys_ref[0, tile : tile + 1, :], (length, length))
        merge = jnp.where(same_group & (across == across.T), 1.0, 0.0).astype(jnp.bfloat16)
        merged = jnp.dot(merge, total, preferred_element_type=jnp.float32)
        out_ref[0, at, :] = merged.astype(jnp.bfloat16)
    out_ref[0, pl.ds(chunk, KEY_ROWS), :] = digits_ref[0]


def spread_blocks(count, values, shifts, keys, parts):
    blocks, length = values.shape
    chunk = blocks // parts
    lines = chunk // length
    keys = keys.reshape(parts, lines, length)
    digits = jnp.stack([keys & 255, (keys >> 8) & 255, keys >> 16], axis=1)
    digits = digits.reshape(parts, 3 * lines, length).astype(jnp.bfloat16)
    digits = jnp.pad(digits, ((0, 0), (0, KEY_ROWS - 3 * lines), (0, 0)))
    return pl.pallas_call(
        spread_kernel,
        grid=(parts,),
        out_shape=jax.ShapeDtypeStruct((parts, chunk + KEY_ROWS, length), jnp.bfloat16),
        in_specs=[
            pl.BlockSpec(memory_space=pltpu.SMEM),
            pl.BlockSpec((chunk, length), lambda i: (i, 0)),
            pl.BlockSpec((chunk, length), lambda i: (i, 0)),
            pl.BlockSpec((1, lines, length), lambda i: (i, 0, 0)),
            pl.BlockSpec((1, KEY_ROWS, length), lambda i: (i, 0, 0)),
        ],
        out_specs=pl.BlockSpec((1, chunk + KEY_ROWS, length), lambda i: (i, 0, 0)),
        name="spread",
    )(count, values, shifts, keys.astype(jnp.float32), digits)


def scatter_kernel(pieces, index_ref, *refs):
    piece_refs, (out_ref, total) = refs[:pieces], refs[pieces:]
    spare = total.shape[0] - 8
    sensors = out_ref.shape[1]
    step = pl.program_id(0)

    @pl.when(step == 0)
    def _():
        def clear(i, carry):
            total[pl.ds(i * 256, 256), :] = jnp.zeros((256, total.shape[1]), jnp.float32)
            return carry

        lax.fori_loop(0, spare // 256, clear, 0)
        total[pl.ds(spare, 8), :] = jnp.zeros((8, total.shape[1]), jnp.float32)
        done = 0
        for piece in piece_refs:
            parts, rows = piece.shape[0], piece.shape[1] - KEY_ROWS
            for part in range(parts):

                def add(i, carry, piece=piece, part=part, base=done):
                    start = i * GROUP
                    places = [index_ref[base + start + j] for j in range(GROUP)]
                    block = piece[part, pl.ds(pl.multiple_of(start, GROUP), GROUP), :]
                    block = block.astype(jnp.float32)
                    sums = [
                        total[pl.ds(places[j], 1), :] + block[j : j + 1, :] for j in range(GROUP)
                    ]
                    for j in range(GROUP):
                        total[pl.ds(places[j], 1), :] = sums[j]
                    return carry

                lax.fori_loop(0, rows // GROUP, add, 0)
                done += rows

    at = pl.ds(pl.multiple_of(step * sensors, sensors), sensors)
    out_ref[0, :, :] = total[at, :].astype(jnp.bfloat16)


def scatter_blocks(index, pieces, owners, panels, sensors):
    length = pieces[0].shape[2]
    rows = owners * panels * sensors
    whole = pl.BlockSpec(pieces[0].shape, lambda i: (0, 0, 0))
    return pl.pallas_call(
        functools.partial(scatter_kernel, len(pieces)),
        grid=(owners * panels,),
        out_shape=jax.ShapeDtypeStruct((owners, sensors, panels * length), jnp.bfloat16),
        in_specs=[pl.BlockSpec(memory_space=pltpu.SMEM)] + [whole] * len(pieces),
        out_specs=pl.BlockSpec((1, sensors, length), lambda i: (i // panels, 0, i % panels)),
        scratch_shapes=[pltpu.VMEM((rows + 8, length), jnp.float32)],
        compiler_params=pltpu.CompilerParams(vmem_limit_bytes=60 << 20),
        name="scatter",
    )(index, *pieces)


def per_device(values, shifts, sensor, window, owner, counts, calibration):
    ring, halves, group_count = lax.axis_size("g"), lax.axis_size("h"), lax.axis_size("col")
    values, shifts = values[0], shifts[0]
    blocks, length = values.shape
    sensors, outputs = calibration.shape
    group_sensors = halves * sensors
    windows = ROWS_DEV // length
    chunk = blocks // group_count
    lines = chunk // length
    my_ring, my_half = lax.axis_index("g"), lax.axis_index("h")

    keys = (owner[0, :, 0] * windows + window[0]) * group_sensors + sensor[0]
    routed = spread_blocks(counts, values, shifts, keys, group_count)
    routed = lax.all_to_all(routed, "col", split_axis=0, concat_axis=0, tiled=True)
    routed = lax.all_to_all(routed, "g", split_axis=0, concat_axis=0, tiled=True)

    def flipped(name, bit):
        return [(i, i ^ bit) for i in range(lax.axis_size(name))]

    def doubled(held, name, bit):
        return held + [lax.ppermute(x, name, flipped(name, bit)) for x in held]

    col_bits = [1 << b for b in reversed(range(1, (group_count - 1).bit_length()))]
    first, second = [routed[: ring // 2]], [routed[ring // 2 :]]
    first = doubled(first, "h", 1)
    for bit in col_bits:
        first, second = doubled(first, "col", bit), doubled(second, "col", bit)
    second = doubled(second, "h", 1)
    pieces = doubled(first, "col", 1) + doubled(second, "col", 1)

    digits = jnp.stack([x[:, chunk : chunk + 3 * lines] for x in pieces])
    digits = digits.reshape(-1, 3, lines, length).astype(jnp.float32).astype(jnp.int32)
    key = (digits[:, 0] + digits[:, 1] * 256 + digits[:, 2] * 65536).reshape(-1)
    to_sensor, to_panel = key % group_sensors, key // group_sensors
    to_owner, to_window = to_panel // windows, to_panel % windows
    to_ring = (to_owner // halves - my_ring + ring) % ring
    panel = (to_ring * halves + to_owner % halves) * windows + to_window
    panels = halves * windows
    index = jnp.where(
        to_sensor // sensors == my_half,
        panel * sensors + to_sensor % sensors,
        ring * panels * sensors,
    )
    aligned = scatter_blocks(index, pieces, ring, panels, sensors)

    def partial(distance):
        return lax.optimization_barrier(
            lax.dot_general(
                aligned[distance % ring],
                calibration,
                (((0,), (0,)), ((), ())),
                preferred_element_type=jnp.float32,
            ).astype(jnp.bfloat16)
        )

    def add(a, b):
        return (a.astype(jnp.float32) + b.astype(jnp.float32)).astype(jnp.bfloat16)

    ahead = [(i, (i + 1) % ring) for i in range(ring)]
    back = [(i, (i - 1) % ring) for i in range(ring)]
    split = outputs // 2
    far = partial(ring // 2)
    up = [lax.ppermute(far[:, :split], "g", ahead)]
    down = [lax.ppermute(far[:, split:], "g", back)]
    for distance in range(ring // 2 - 1, 0, -1):
        rise, fall = partial(distance), partial(-distance)
        rise_parts, fall_parts = [rise[:, :split], rise[:, split:]], [fall[:, split:], fall[:, :split]]
        up = [lax.ppermute(add(rise_parts[i], up[i]) if i < len(up) else rise_parts[i], "g", ahead) for i in range(2)]
        down = [lax.ppermute(add(fall_parts[i], down[i]) if i < len(down) else fall_parts[i], "g", back) for i in range(2)]
    here = partial(0)
    total = (
        here.astype(jnp.float32)
        + jnp.concatenate(up, axis=1).astype(jnp.float32)
        + jnp.concatenate(down[::-1], axis=1).astype(jnp.float32)
    )
    total = total.astype(jnp.bfloat16).reshape(halves, ROWS_DEV, outputs)
    mine = lax.dynamic_index_in_dim(total, my_half, 0, keepdims=False)
    other = lax.dynamic_index_in_dim(total, 1 - my_half, 0, keepdims=False)
    return add(mine, lax.ppermute(other, "h", flipped("h", 1)))


def solution(mesh):
    rows, cols = mesh.devices.shape
    if rows != 2 * cols:
        raise ValueError("mesh shape")
    split_mesh = Mesh(mesh.devices.reshape(cols, 2, cols), ("g", "h", "col"))
    time = ("g", "h")
    placed = (
        P("col", time, None),
        P("col", time, None),
        P("col", time),
        P("col", time),
        P("col", time, None),
        P("col", time),
        P(time, "col"),
    )
    return jax.shard_map(
        per_device, mesh=split_mesh, in_specs=placed, out_specs=P(time, "col"), check_vma=False
    )
```

time: 894 us -> 307 us (0.34)
  blocking collectives: 369 us -> 33.6 us
  waiting for transfers between devices: 288 us -> 166 us
  matrix products: 121 us -> 24.9 us
  Pallas kernels: 0 us -> 51.7 us
  local copies, waits for them, and re-layouts: 44 us -> 2.14 us
  other arithmetic: 39.2 us -> 8.13 us
  between operations: 14.7 us -> 1.08 us
    all_to_all x1 -> x2, blocking collectives: 369 us -> 33.6 us  [the longest x1 20.4 us: per_device(): lax.all_to_all(routed, 'g', split_axis=0, concat_axis=0, tiled=True)]
    ppermute x0 -> x21, waiting for transfers between devices: none -> 166 us  [the longest x1 39.3 us: per_device(): down = [lax.ppermute(far[:, split:], 'g', back)]]
    reduce_scatter x1 -> x0, waiting for transfers between devices: 146 us -> none  [per_device(): lax.psum_scatter(jnp.dot(regrouped, calibration, preferred_element_type=j...]
    all_gather x1 -> x0, waiting for transfers between devices: 105 us -> none  [per_device(): gathered = lax.all_gather(aligned, 'col', axis=1, tiled=True)]
    dot_general x10 -> x4, matrix products: 121 us -> 24.9 us  [partial(): lax.dot_general(aligned[distance % ring], calibration, (((0,), (0,)), (()...]
    pallas_call x0 -> x2, Pallas kernels: none -> 51.7 us  [the longest x1 47.5 us: scatter_blocks(): pl.pallas_call(functools.partial(scatter_kernel, len(pieces)), grid=(owne...]
    all_to_all x2 -> x0, waiting for transfers between devices: 36.4 us -> none  [the longest x1 36.4 us: per_device(): lax.all_to_all(outgoing, 'tm', split_axis=0, concat_axis=0, tiled=True)]
    gather x2 -> x0, local copies, waits for them, and re-layouts: 27.8 us -> none  [the longest x1 17.4 us: per_device(): jnp.take(row_keys, source_row, axis=0)]
  transfers between devices with their start and end apart: 4 -> 21, of which waited for: 3 -> 12; matrix products, arithmetic and copies ran while one was open for 5% -> 4% of each run, Pallas kernels for 0% -> 0%
where the time goes in v1:
time: 307 us; the launch traced here: 306 us
  waiting for transfers between devices  166 us (54%)
  Pallas kernels  51.7 us (17%)
  blocking collectives  33.6 us (11%)
  matrix products  24.9 us (8%)
  starting transfers between devices  18.4 us (6%)
  other arithmetic  8.13 us (3%)
    pallas_call x1, Pallas kernels, scatter_blocks(): pl.pallas_call(functools.partial(scatter_kernel, len(pieces)), grid=(owne...  47.5 us
    ppermute x1, waiting for transfers between devices, per_device(): down = [lax.ppermute(far[:, split:], 'g', back)]  39.3 us
    ppermute x2, waiting for transfers between devices, per_device(): lax.ppermute(add(rise_parts[i], up[i]) if i < len(up) else rise_parts[i],...  37.4 us
    ppermute x14, waiting for transfers between devices, doubled(): return held + [lax.ppermute(x, name, flipped(name, bit)) for x in held]  25.3 us
    dot_general x4, matrix products, partial(): lax.dot_general(aligned[distance % ring], calibration, (((0,), (0,)), (()...  24.9 us
    ppermute x1, waiting for transfers between devices, per_device(): return add(mine, lax.ppermute(other, 'h', flipped('h', 1)))  22.9 us
    ppermute x2, waiting for transfers between devices, per_device(): lax.ppermute(add(fall_parts[i], down[i]) if i < len(down) else fall_parts...  22.5 us
    all_to_all x1, blocking collectives, per_device(): lax.all_to_all(routed, 'g', split_axis=0, concat_axis=0, tiled=True)  20.4 us
  transfers between devices with their start and end apart: 21, of which 12 were waited for; matrix products, arithmetic and copies ran while one was open for 4% of the time, Pallas kernels for 0%

profile of v1, /device:TPU:0, one launch (start us, length us, event | category | flops | bytes accessed | tf_op | source)
XLA Modules:
  0.0 306.0 jit_solution(9152262461613787701)
XLA Ops:
  0.7 0.7 broadcast_multiply_fusion
  1.4 0.7 and_convert_fusion.1
  2.1 0.6 pad.4.digits_ref
  2.7 1.3 add_convert_fusion.3.keys_ref
  4.1 4.2 %spread.1 = bf16[4,528,128]{2,1,0:T(8,128)(2,1)} custom-call(s32[1,1]{1,0:T(1,128)S(6)} %copy.53.count_ref, bf16[2048,128]{1,0:T(8,128)(2,1)} %bitcast.110, bf16[2048,128]{1,0:T(8,128)(2,1)} %bitcast.111, f32[4,4,128]{2,1,0:T(4,128)} %add_convert_fusion.3.keys_ref, bf16[4,16,128]{2,1,0:T(8,128)(2,1)} %pad.4.digits_ref), custom_call_target="tpu_custom_call" | custom-call | tf_op jit(solution)/shard_map/spread/pallas_call | solution.py:50
  8.3 13.2 %all_to_all.10 = bf16[4,528,128]{2,1,0:T(8,128)(2,1)S(1)} all-to-all(bf16[4,528,128]{2,1,0:T(8,128)(2,1)} %spread.1), channel_id=1, replica_groups=mesh['g'=4,'h'=2,'col'=4] {'col'}, dimensions={0} | all-to-all | bytes 1081344 | tf_op jit(solution)/shard_map/all_to_all | solution.py:133
  21.5 20.4 %all_to_all.11 = bf16[4,528,128]{2,1,0:T(8,128)(2,1)S(1)} all-to-all(bf16[4,528,128]{2,1,0:T(8,128)(2,1)S(1)} %all_to_all.10), channel_id=1, replica_groups=mesh['g'=4,'h'=2,'col'=4] {'g'}, dimensions={0} | all-to-all | bytes 1081344 | tf_op jit(solution)/shard_map/all_to_all | solution.py:134
  41.9 0.0 copy-start.1
  41.9 1.6 collective-permute-start
  43.5 0.0 collective-permute-start.10
  43.5 0.5 collective-permute-start.8
  44.0 0.4 collective-permute-start.7
  44.4 1.6 collective-permute-start.1
  46.0 5.3 %collective-permute-done.refs_1_ = bf16[2,528,128]{2,1,0:T(8,128)(2,1)S(1)} collective-permute-done((bf16[2,528,128]{2,1,0:T(8,128)(2,1)S(1)}, bf16[2,528,128]{2,1,0:T(8,128)(2,1)S(1)}, u32[]{:S(2)}, u32[]{:S(2)}) %collective-permute-start) | collective-permute-done | bytes 270368 | tf_op jit(solution)/shard_map/ppermute | solution.py:140
  51.3 0.4 collective-permute-start.2
  51.7 7.4 %collective-permute-done.1.refs_2_ = bf16[2,528,128]{2,1,0:T(8,128)(2,1)S(1)} collective-permute-done((bf16[2,528,128]{2,1,0:T(8,128)(2,1)S(1)}, bf16[2,528,128]{2,1,0:T(8,128)(2,1)S(1)}, u32[]{:S(2)}, u32[]{:S(2)}) %collective-permute-start.1) | collective-permute-done | bytes 270368 | tf_op jit(solution)/shard_map/ppermute | solution.py:140
  59.2 0.0 collective-permute-start.3
  59.2 5.0 %collective-permute-done.2.refs_3_ = bf16[2,528,128]{2,1,0:T(8,128)(2,1)S(1)} collective-permute-done((bf16[2,528,128]{2,1,0:T(8,128)(2,1)S(1)}, bf16[2,528,128]{2,1,0:T(8,128)(2,1)S(1)}, u32[]{:S(2)}, u32[]{:S(2)}) %collective-permute-start.2) | collective-permute-done | bytes 270368 | tf_op jit(solution)/shard_map/ppermute | solution.py:140
  64.2 0.6 collective-permute-start.5
  64.8 0.0 collective-permute-done.3.refs_4_
  64.8 1.5 collective-permute-start.9
  66.3 0.1 collective-permute-start.6
  66.4 0.0 collective-permute-done.8.refs_10_
  66.5 0.5 collective-permute-start.11
  67.0 6.3 %collective-permute-done.9.refs_11_ = bf16[2,528,128]{2,1,0:T(8,128)(2,1)S(1)} collective-permute-done((bf16[2,528,128]{2,1,0:T(8,128)(2,1)S(1)}, bf16[2,528,128]{2,1,0:T(8,128)(2,1)S(1)}, u32[]{:S(2)}, u32[]{:S(2)}) %collective-permute-start.9) | collective-permute-done | bytes 270368 | tf_op jit(solution)/shard_map/ppermute | solution.py:140
  73.3 0.0 collective-permute-start.12
  73.3 0.0 collective-permute-done.5.refs_6_
  73.3 0.5 collective-permute-start.13
  73.8 0.0 collective-permute-done.6.refs_7_
  73.9 0.0 collective-permute-done.10.refs_12_
  73.9 0.0 collective-permute-done.11.refs_13_
  73.9 0.9 collective-permute-done.12.refs_14_
  74.9 0.4 collective-permute-done.13.refs_15_
  75.2 0.3 copy-done.14
  75.5 0.4 copy-done.15
  76.0 0.1 copy.26
  76.2 0.9 fusion.19.index_ref
  77.2 47.5 %scatter.1 = bf16[4,2048,1024]{2,1,0:T(8,128)(2,1)} custom-call(s32[16384]{0:T(1024)} %fusion.19.index_ref, bf16[2,528,128]{2,1,0:T(8,128)(2,1)} %copy-done.1, bf16[2,528,128]{2,1,0:T(8,128)(2,1)} %copy-done.2, bf16[2,528,128]{2,1,0:T(8,128)(2,1)} %copy-done.6, bf16[2,528,128]{2,1,0:T(8,128)(2,1)} %copy-done.7, bf16[2,528,128]{2,1,0:T(8,128)(2,1)} %copy-done.8, ...), custom_call_target="tpu_custom_call" | custom-call | tf_op jit(solution)/shard_map/scatter/pallas_call | solution.py:108
  124.7 0.0 slice-start.1
  124.7 8.2 %fusion.8 = bf16[1024,1024]{1,0:T(8,128)(2,1)S(1)} fusion(bf16[2048,1024]{1,0:T(8,128)(2,1)} %param.13, bf16[4,2048,1024]{2,1,0:T(8,128)(2,1)} %scatter.1), kind=kOutput, calls=%fused_computation.16 | convolution fusion | flops 4296015872 | bytes 10485760 | tf_op jit(solution)/shard_map/dot_general | solution.py:167
  132.9 7.2 %fusion.7 = bf16[1024,1024]{1,0:T(8,128)(2,1)S(1)} fusion(bf16[2048,1024]{1,0:T(8,128)(2,1)S(1)} %copy-done.16, bf16[4,2048,1024]{2,1,0:T(8,128)(2,1)} %scatter.1), kind=kOutput, calls=%fused_computation.15 | convolution fusion | flops 4296015872 | bytes 10485760 | tf_op jit(solution)/shard_map/dot_general | solution.py:167
  140.1 0.1 slice.154
  140.2 1.5 collective-permute-start.17
  141.7 0.2 fusion.29
  141.9 0.6 collective-permute-start.18
  142.5 1.5 collective-permute-start.14
  144.0 4.8 %fusion.6 = bf16[1024,1024]{1,0:T(8,128)(2,1)S(1)} fusion(bf16[2048,1024]{1,0:T(8,128)(2,1)S(1)} %copy-done.16, bf16[4,2048,1024]{2,1,0:T(8,128)(2,1)S(1)} %bitcast.106), kind=kOutput, calls=%fused_computation.14 | convolution fusion | flops 4296015872 | bytes 10485760 | tf_op jit(solution)/shard_map/dot_general | solution.py:167
  148.8 0.1 slice.152
  148.9 0.6 collective-permute-start.16
  149.5 39.3 %collective-permute-done.18 = bf16[1024,512]{1,0:T(8,128)(2,1)S(1)} collective-permute-done((bf16[1024,512]{1,0:T(8,128)(2,1)S(1)}, bf16[1024,512]{1,0:T(8,128)(2,1)S(1)}, u32[]{:S(2)}, u32[]{:S(2)}) %collective-permute-start.18) | collective-permute-done | bytes 1048608 | tf_op jit(solution)/shard_map/ppermute | solution.py:183
  188.8 0.4 add_convert_fusion.1
  189.2 3.4 %collective-permute-start.19 = (bf16[1024,512]{1,0:T(8,128)(2,1)S(1)}, bf16[1024,512]{1,0:T(8,128)(2,1)S(1)}, u32[]{:S(2)}, u32[]{:S(2)}) collective-permute-start(bf16[1024,512]{1,0:T(8,128)(2,1)S(1)} %add_convert_fusion.1), channel_id=1, source_target_pairs={{0,24},{8,0},{16,8},{24,16},{1,25},{9,1},{17,9},{25,17},{2,26},{10... | collective-permute-start | bytes 3145736 | tf_op jit(solution)/shard_map/ppermute | solution.py:188
  192.5 18.7 %collective-permute-done.14 = bf16[1024,512]{1,0:T(8,128)(2,1)S(1)} collective-permute-done((bf16[1024,512]{1,0:T(8,128)(2,1)S(1)}, bf16[1024,512]{1,0:T(8,128)(2,1)S(1)}, u32[]{:S(2)}, u32[]{:S(2)}) %collective-permute-start.14) | collective-permute-done | bytes 1048608 | tf_op jit(solution)/shard_map/ppermute | solution.py:182
  211.3 0.4 add_convert_fusion.2
  211.7 1.5 collective-permute-start.15
  213.2 4.8 %fusion.5 = bf16[1024,1024]{1,0:T(8,128)(2,1)S(1)} fusion(bf16[2048,1024]{1,0:T(8,128)(2,1)S(1)} %copy-done.16, bf16[4,2048,1024]{2,1,0:T(8,128)(2,1)S(1)} %bitcast.106), kind=kOutput, calls=%fused_computation.13 | convolution fusion | flops 4296015872 | bytes 10485760 | tf_op jit(solution)/shard_map/dot_general | solution.py:167
  218.0 15.7 %collective-permute-done.16 = bf16[1024,512]{1,0:T(8,128)(2,1)S(1)} collective-permute-done((bf16[1024,512]{1,0:T(8,128)(2,1)S(1)}, bf16[1024,512]{1,0:T(8,128)(2,1)S(1)}, u32[]{:S(2)}, u32[]{:S(2)}) %collective-permute-start.16) | collective-permute-done | bytes 1048608 | tf_op jit(solution)/shard_map/ppermute | solution.py:187
  233.7 22.5 %collective-permute-done.19 = bf16[1024,512]{1,0:T(8,128)(2,1)S(1)} collective-permute-done((bf16[1024,512]{1,0:T(8,128)(2,1)S(1)}, bf16[1024,512]{1,0:T(8,128)(2,1)S(1)}, u32[]{:S(2)}, u32[]{:S(2)}) %collective-permute-start.19) | collective-permute-done | bytes 1048608 | tf_op jit(solution)/shard_map/ppermute | solution.py:188
  256.2 21.7 %collective-permute-done.15 = bf16[1024,512]{1,0:T(8,128)(2,1)S(1)} collective-permute-done((bf16[1024,512]{1,0:T(8,128)(2,1)S(1)}, bf16[1024,512]{1,0:T(8,128)(2,1)S(1)}, u32[]{:S(2)}, u32[]{:S(2)}) %collective-permute-start.15) | collective-permute-done | bytes 1048608 | tf_op jit(solution)/shard_map/ppermute | solution.py:187
  277.8 1.0 add_convert_fusion
  278.8 0.1 dynamic-slice_bitcast_fusion
  278.9 1.6 collective-permute-start.20
  280.5 22.9 %collective-permute-done.20 = bf16[512,1024]{1,0:T(8,128)(2,1)} collective-permute-done((bf16[512,1024]{1,0:T(8,128)(2,1)S(1)}, bf16[512,1024]{1,0:T(8,128)(2,1)}, u32[]{:S(2)}, u32[]{:S(2)}) %collective-permute-start.20) | collective-permute-done | bytes 1048608 | tf_op jit(solution)/shard_map/ppermute | solution.py:198
  303.4 2.6 fusion.4
  (66 shorter events, 0.4 us)
Async XLA Ops:
  41.9 35.2 %copy-start = (bf16[2,528,128]{2,1,0:T(8,128)(2,1)}, bf16[2,528,128]{2,1,0:T(8,128)(2,1)S(1)}, u32[]{:S(2)}) copy-start(bf16[2,528,128]{2,1,0:T(8,128)(2,1)S(1)} %get-tuple-element.9.refs_8_) | copy-start | bytes 811012
  41.9 35.2 %copy-start.1 = (bf16[2,528,128]{2,1,0:T(8,128)(2,1)}, bf16[2,528,128]{2,1,0:T(8,128)(2,1)S(1)}, u32[]{:S(2)}) copy-start(bf16[2,528,128]{2,1,0:T(8,128)(2,1)S(1)} %get-tuple-element.10.refs_0_) | copy-start | bytes 811012
  41.9 9.4 %collective-permute-start = (bf16[2,528,128]{2,1,0:T(8,128)(2,1)S(1)}, bf16[2,528,128]{2,1,0:T(8,128)(2,1)S(1)}, u32[]{:S(2)}, u32[]{:S(2)}) collective-permute-start(bf16[2,528,128]{2,1,0:T(8,128)(2,1)S(1)} %get-tuple-element.10.refs_0_), channel_id=1, source_target_pairs={{0,4},{4,0},{1,5},{5,1},{2,6},{6,2},{3,7},{7,3},{8,12},{12,8},{9,1... | collective-permute-start | bytes 811016 | tf_op jit(solution)/shard_map/ppermute | solution.py:140
  43.5 30.4 %collective-permute-start.10 = (bf16[2,528,128]{2,1,0:T(8,128)(2,1)S(1)}, bf16[2,528,128]{2,1,0:T(8,128)(2,1)S(1)}, u32[]{:S(2)}, u32[]{:S(2)}) collective-permute-start(bf16[2,528,128]{2,1,0:T(8,128)(2,1)S(1)} %get-tuple-element.9.refs_8_), channel_id=1, source_target_pairs={{0,1},{1,0},{2,3},{3,2},{4,5},{5,4},{6,7},{7,6},{8,9},{9,8},{10,11... | collective-permute-start | bytes 811016 | tf_op jit(solution)/shard_map/ppermute | solution.py:140
  43.5 22.9 %collective-permute-start.8 = (bf16[2,528,128]{2,1,0:T(8,128)(2,1)S(1)}, bf16[2,528,128]{2,1,0:T(8,128)(2,1)S(1)}, u32[]{:S(2)}, u32[]{:S(2)}) collective-permute-start(bf16[2,528,128]{2,1,0:T(8,128)(2,1)S(1)} %get-tuple-element.9.refs_8_), channel_id=1, source_target_pairs={{0,4},{4,0},{1,5},{5,1},{2,6},{6,2},{3,7},{7,3},{8,12},{12,8},{9,1... | collective-permute-start | bytes 811016 | tf_op jit(solution)/shard_map/ppermute | solution.py:140
  44.0 20.2 %collective-permute-start.7 = (bf16[2,528,128]{2,1,0:T(8,128)(2,1)S(1)}, bf16[2,528,128]{2,1,0:T(8,128)(2,1)S(1)}, u32[]{:S(2)}, u32[]{:S(2)}) collective-permute-start(bf16[2,528,128]{2,1,0:T(8,128)(2,1)S(1)} %get-tuple-element.9.refs_8_), channel_id=1, source_target_pairs={{0,2},{1,3},{2,0},{3,1},{4,6},{5,7},{6,4},{7,5},{8,10},{9,11},{10,... | collective-permute-start | bytes 811016 | tf_op jit(solution)/shard_map/ppermute | solution.py:140
  44.4 14.8 %collective-permute-start.1 = (bf16[2,528,128]{2,1,0:T(8,128)(2,1)S(1)}, bf16[2,528,128]{2,1,0:T(8,128)(2,1)S(1)}, u32[]{:S(2)}, u32[]{:S(2)}) collective-permute-start(bf16[2,528,128]{2,1,0:T(8,128)(2,1)S(1)} %get-tuple-element.10.refs_0_), channel_id=1, source_target_pairs={{0,2},{1,3},{2,0},{3,1},{4,6},{5,7},{6,4},{7,5},{8,10},{9,11},{10,... | collective-permute-start | bytes 811016 | tf_op jit(solution)/shard_map/ppermute | solution.py:140
  51.3 25.7 %copy-start.2 = (bf16[2,528,128]{2,1,0:T(8,128)(2,1)}, bf16[2,528,128]{2,1,0:T(8,128)(2,1)S(1)}, u32[]{:S(2)}) copy-start(bf16[2,528,128]{2,1,0:T(8,128)(2,1)S(1)} %collective-permute-done.refs_1_) | copy-start | bytes 811012
  51.3 12.9 %collective-permute-start.2 = (bf16[2,528,128]{2,1,0:T(8,128)(2,1)S(1)}, bf16[2,528,128]{2,1,0:T(8,128)(2,1)S(1)}, u32[]{:S(2)}, u32[]{:S(2)}) collective-permute-start(bf16[2,528,128]{2,1,0:T(8,128)(2,1)S(1)} %collective-permute-done.refs_1_), channel_id=1, source_target_pairs={{0,2},{1,3},{2,0},{3,1},{4,6},{5,7},{6,4},{7,5},{8,10},{9,11},{10,... | collective-permute-start | bytes 811016 | tf_op jit(solution)/shard_map/ppermute | solution.py:140
  59.2 17.9 %copy-start.6 = (bf16[2,528,128]{2,1,0:T(8,128)(2,1)}, bf16[2,528,128]{2,1,0:T(8,128)(2,1)S(1)}, u32[]{:S(2)}) copy-start(bf16[2,528,128]{2,1,0:T(8,128)(2,1)S(1)} %collective-permute-done.1.refs_2_) | copy-start | bytes 811012
  59.2 5.6 %collective-permute-start.3 = (bf16[2,528,128]{2,1,0:T(8,128)(2,1)S(1)}, bf16[2,528,128]{2,1,0:T(8,128)(2,1)S(1)}, u32[]{:S(2)}, u32[]{:S(2)}) collective-permute-start(bf16[2,528,128]{2,1,0:T(8,128)(2,1)S(1)} %get-tuple-element.10.refs_0_), channel_id=1, source_target_pairs={{0,1},{1,0},{2,3},{3,2},{4,5},{5,4},{6,7},{7,6},{8,9},{9,8},{10,11... | collective-permute-start | bytes 811016 | tf_op jit(solution)/shard_map/ppermute | solution.py:140
  64.2 12.9 %copy-start.7 = (bf16[2,528,128]{2,1,0:T(8,128)(2,1)}, bf16[2,528,128]{2,1,0:T(8,128)(2,1)S(1)}, u32[]{:S(2)}) copy-start(bf16[2,528,128]{2,1,0:T(8,128)(2,1)S(1)} %collective-permute-done.2.refs_3_) | copy-start | bytes 811012
  64.2 2.1 collective-permute-start.4
  64.2 12.9 %copy-start.5 = (bf16[2,528,128]{2,1,0:T(8,128)(2,1)}, bf16[2,528,128]{2,1,0:T(8,128)(2,1)S(1)}, u32[]{:S(2)}) copy-start(bf16[2,528,128]{2,1,0:T(8,128)(2,1)S(1)} %collective-permute-done.7.refs_9_) | copy-start | bytes 811012
  64.2 9.1 %collective-permute-start.5 = (bf16[2,528,128]{2,1,0:T(8,128)(2,1)S(1)}, bf16[2,528,128]{2,1,0:T(8,128)(2,1)S(1)}, u32[]{:S(2)}, u32[]{:S(2)}) collective-permute-start(bf16[2,528,128]{2,1,0:T(8,128)(2,1)S(1)} %collective-permute-done.1.refs_2_), channel_id=1, source_target_pairs={{0,1},{1,0},{2,3},{3,2},{4,5},{5,4},{6,7},{7,6},{8,9},{9,8},{10,11... | collective-permute-start | bytes 811016 | tf_op jit(solution)/shard_map/ppermute | solution.py:140
  64.8 12.3 %copy-start.8 = (bf16[2,528,128]{2,1,0:T(8,128)(2,1)}, bf16[2,528,128]{2,1,0:T(8,128)(2,1)S(1)}, u32[]{:S(2)}) copy-start(bf16[2,528,128]{2,1,0:T(8,128)(2,1)S(1)} %collective-permute-done.3.refs_4_) | copy-start | bytes 811012
  64.8 8.5 %collective-permute-start.9 = (bf16[2,528,128]{2,1,0:T(8,128)(2,1)S(1)}, bf16[2,528,128]{2,1,0:T(8,128)(2,1)S(1)}, u32[]{:S(2)}, u32[]{:S(2)}) collective-permute-start(bf16[2,528,128]{2,1,0:T(8,128)(2,1)S(1)} %collective-permute-done.7.refs_9_), channel_id=1, source_target_pairs={{0,4},{4,0},{1,5},{5,1},{2,6},{6,2},{3,7},{7,3},{8,12},{12,8},{9,1... | collective-permute-start | bytes 811016 | tf_op jit(solution)/shard_map/ppermute | solution.py:140
  66.3 10.8 %copy-start.9 = (bf16[2,528,128]{2,1,0:T(8,128)(2,1)}, bf16[2,528,128]{2,1,0:T(8,128)(2,1)S(1)}, u32[]{:S(2)}) copy-start(bf16[2,528,128]{2,1,0:T(8,128)(2,1)S(1)} %collective-permute-done.4.refs_5_) | copy-start | bytes 811012
  66.3 7.5 %collective-permute-start.6 = (bf16[2,528,128]{2,1,0:T(8,128)(2,1)S(1)}, bf16[2,528,128]{2,1,0:T(8,128)(2,1)S(1)}, u32[]{:S(2)}, u32[]{:S(2)}) collective-permute-start(bf16[2,528,128]{2,1,0:T(8,128)(2,1)S(1)} %collective-permute-done.2.refs_3_), channel_id=1, source_target_pairs={{0,1},{1,0},{2,3},{3,2},{4,5},{5,4},{6,7},{7,6},{8,9},{9,8},{10,11... | collective-permute-start | bytes 811016 | tf_op jit(solution)/shard_map/ppermute | solution.py:140
  66.4 10.7 %copy-start.4 = (bf16[2,528,128]{2,1,0:T(8,128)(2,1)}, bf16[2,528,128]{2,1,0:T(8,128)(2,1)S(1)}, u32[]{:S(2)}) copy-start(bf16[2,528,128]{2,1,0:T(8,128)(2,1)S(1)} %collective-permute-done.8.refs_10_) | copy-start | bytes 811012
  66.5 7.5 %collective-permute-start.11 = (bf16[2,528,128]{2,1,0:T(8,128)(2,1)S(1)}, bf16[2,528,128]{2,1,0:T(8,128)(2,1)S(1)}, u32[]{:S(2)}, u32[]{:S(2)}) collective-permute-start(bf16[2,528,128]{2,1,0:T(8,128)(2,1)S(1)} %collective-permute-done.7.refs_9_), channel_id=1, source_target_pairs={{0,1},{1,0},{2,3},{3,2},{4,5},{5,4},{6,7},{7,6},{8,9},{9,8},{10,11... | collective-permute-start | bytes 811016 | tf_op jit(solution)/shard_map/ppermute | solution.py:140
  73.3 3.8 %copy-start.11 = (bf16[2,528,128]{2,1,0:T(8,128)(2,1)}, bf16[2,528,128]{2,1,0:T(8,128)(2,1)S(1)}, u32[]{:S(2)}) copy-start(bf16[2,528,128]{2,1,0:T(8,128)(2,1)S(1)} %collective-permute-done.9.refs_11_) | copy-start | bytes 811012
  73.3 1.5 collective-permute-start.12
  73.3 3.8 %copy-start.10 = (bf16[2,528,128]{2,1,0:T(8,128)(2,1)}, bf16[2,528,128]{2,1,0:T(8,128)(2,1)S(1)}, u32[]{:S(2)}) copy-start(bf16[2,528,128]{2,1,0:T(8,128)(2,1)S(1)} %collective-permute-done.5.refs_6_) | copy-start | bytes 811012
  73.3 1.9 collective-permute-start.13
  73.8 3.3 %copy-start.12 = (bf16[2,528,128]{2,1,0:T(8,128)(2,1)}, bf16[2,528,128]{2,1,0:T(8,128)(2,1)S(1)}, u32[]{:S(2)}) copy-start(bf16[2,528,128]{2,1,0:T(8,128)(2,1)S(1)} %collective-permute-done.6.refs_7_) | copy-start | bytes 811012
  73.9 3.3 %copy-start.3 = (bf16[2,528,128]{2,1,0:T(8,128)(2,1)}, bf16[2,528,128]{2,1,0:T(8,128)(2,1)S(1)}, u32[]{:S(2)}) copy-start(bf16[2,528,128]{2,1,0:T(8,128)(2,1)S(1)} %collective-permute-done.10.refs_12_) | copy-start | bytes 811012
  73.9 1.3 copy-start.13
  74.8 0.7 copy-start.14
  75.2 0.7 copy-start.15
  124.7 8.2 %copy-start.16 = (bf16[2048,1024]{1,0:T(8,128)(2,1)S(1)}, bf16[2048,1024]{1,0:T(8,128)(2,1)}, u32[]{:S(2)}) copy-start(bf16[2048,1024]{1,0:T(8,128)(2,1)} %param.13) | copy-start | bytes 12582916
  124.7 19.3 %slice-start = ((s8[16777216]{0:T(1024)(128)(4,1)}), s8[4194304]{0:T(1024)(128)(4,1)S(1)}, s32[]{:S(2)}) async-start(s8[16777216]{0:T(1024)(128)(4,1)} %bitcast.105), calls=%async_computation.2 | async-start | bytes 8388608
  124.7 19.3 %slice-start.1 = ((s8[16777216]{0:T(1024)(128)(4,1)}), s8[4194304]{0:T(1024)(128)(4,1)S(1)}, s32[]{:S(2)}) async-start(s8[16777216]{0:T(1024)(128)(4,1)} %bitcast.105), calls=%async_computation.3 | async-start | bytes 8388608
  132.9 11.1 %slice-start.2 = ((s8[16777216]{0:T(1024)(128)(4,1)}), s8[4194304]{0:T(1024)(128)(4,1)S(1)}, s32[]{:S(2)}) async-start(s8[16777216]{0:T(1024)(128)(4,1)} %bitcast.105), calls=%async_computation.4 | async-start | bytes 8388608
  132.9 11.1 %slice-start.3 = ((s8[16777216]{0:T(1024)(128)(4,1)}), s8[4194304]{0:T(1024)(128)(4,1)S(1)}, s32[]{:S(2)}) async-start(s8[16777216]{0:T(1024)(128)(4,1)} %bitcast.105), calls=%async_computation.5 | async-start | bytes 8388608
  140.2 77.8 %collective-permute-start.17 = (bf16[1024,512]{1,0:T(8,128)(2,1)S(1)}, bf16[1024,512]{1,0:T(8,128)(2,1)S(1)}, u32[]{:S(2)}, u32[]{:S(2)}) collective-permute-start(bf16[1024,512]{1,0:T(8,128)(2,1)S(1)} %slice.154), channel_id=1, source_target_pairs={{0,24},{8,0},{16,8},{24,16},{1,25},{9,1},{17,9},{25,17},{2,26},{10... | collective-permute-start | bytes 3145736 | tf_op jit(solution)/shard_map/ppermute | solution.py:188
  141.9 46.9 %collective-permute-start.18 = (bf16[1024,512]{1,0:T(8,128)(2,1)S(1)}, bf16[1024,512]{1,0:T(8,128)(2,1)S(1)}, u32[]{:S(2)}, u32[]{:S(2)}) collective-permute-start(bf16[1024,512]{1,0:T(8,128)(2,1)S(1)} %get-tuple-element.7), channel_id=1, source_target_pairs={{0,24},{8,0},{16,8},{24,16},{1,25},{9,1},{17,9},{25,17},{2,26},{10... | collective-permute-start | bytes 3145736 | tf_op jit(solution)/shard_map/ppermute | solution.py:183
  142.5 68.8 %collective-permute-start.14 = (bf16[1024,512]{1,0:T(8,128)(2,1)S(1)}, bf16[1024,512]{1,0:T(8,128)(2,1)S(1)}, u32[]{:S(2)}, u32[]{:S(2)}) collective-permute-start(bf16[1024,512]{1,0:T(8,128)(2,1)S(1)} %get-tuple-element.8), channel_id=1, source_target_pairs={{0,8},{8,16},{16,24},{24,0},{1,9},{9,17},{17,25},{25,1},{2,10},{10... | collective-permute-start | bytes 3145736 | tf_op jit(solution)/shard_map/ppermute | solution.py:182
  148.9 84.8 %collective-permute-start.16 = (bf16[1024,512]{1,0:T(8,128)(2,1)S(1)}, bf16[1024,512]{1,0:T(8,128)(2,1)S(1)}, u32[]{:S(2)}, u32[]{:S(2)}) collective-permute-start(bf16[1024,512]{1,0:T(8,128)(2,1)S(1)} %slice.152), channel_id=1, source_target_pairs={{0,8},{8,16},{16,24},{24,0},{1,9},{9,17},{17,25},{25,1},{2,10},{10... | collective-permute-start | bytes 3145736 | tf_op jit(solution)/shard_map/ppermute | solution.py:187
  189.2 67.0 %collective-permute-start.19 = (bf16[1024,512]{1,0:T(8,128)(2,1)S(1)}, bf16[1024,512]{1,0:T(8,128)(2,1)S(1)}, u32[]{:S(2)}, u32[]{:S(2)}) collective-permute-start(bf16[1024,512]{1,0:T(8,128)(2,1)S(1)} %add_convert_fusion.1), channel_id=1, source_target_pairs={{0,24},{8,0},{16,8},{24,16},{1,25},{9,1},{17,9},{25,17},{2,26},{10... | collective-permute-start | bytes 3145736 | tf_op jit(solution)/shard_map/ppermute | solution.py:188
  211.7 66.1 %collective-permute-start.15 = (bf16[1024,512]{1,0:T(8,128)(2,1)S(1)}, bf16[1024,512]{1,0:T(8,128)(2,1)S(1)}, u32[]{:S(2)}, u32[]{:S(2)}) collective-permute-start(bf16[1024,512]{1,0:T(8,128)(2,1)S(1)} %add_convert_fusion.2), channel_id=1, source_target_pairs={{0,8},{8,16},{16,24},{24,0},{1,9},{9,17},{17,25},{25,1},{2,10},{10... | collective-permute-start | bytes 3145736 | tf_op jit(solution)/shard_map/ppermute | solution.py:187
  278.9 24.5 %collective-permute-start.20 = (bf16[512,1024]{1,0:T(8,128)(2,1)S(1)}, bf16[512,1024]{1,0:T(8,128)(2,1)}, u32[]{:S(2)}, u32[]{:S(2)}) collective-permute-start(bf16[512,1024]{1,0:T(8,128)(2,1)S(1)} %dynamic-slice_bitcast_fusion), channel_id=1, source_target_pairs={{0,4},{4,0},{1,5},{5,1},{2,6},{6,2},{3,7},{7,3},{8,12},{12,8},{9,1... | collective-permute-start | bytes 3145736 | tf_op jit(solution)/shard_map/ppermute | solution.py:198

commit v2 on v1

--- a/solution.py
+++ b/solution.py
@@ -10,6 +10,7 @@
 ROWS_DEV = 512
 GROUP = 16
 KEY_ROWS = 16
+CHUNKS = 2
 
 
 def spread_kernel(count_ref, values_ref, shifts_ref, keys_ref, digits_ref, out_ref):
@@ -128,13 +129,17 @@
     lines = chunk // length
     my_ring, my_half = lax.axis_index("g"), lax.axis_index("h")
 
+    def flipped(name, bit):
+        return [(i, i ^ bit) for i in range(lax.axis_size(name))]
+
+    split = outputs // CHUNKS
+    own_parts = [calibration[:, i * split : (i + 1) * split] for i in range(CHUNKS)]
+    other_parts = [lax.ppermute(own_parts[0], "h", flipped("h", 1))]
+
     keys = (owner[0, :, 0] * windows + window[0]) * group_sensors + sensor[0]
     routed = spread_blocks(counts, values, shifts, keys, group_count)
     routed = lax.all_to_all(routed, "col", split_axis=0, concat_axis=0, tiled=True)
     routed = lax.all_to_all(routed, "g", split_axis=0, concat_axis=0, tiled=True)
-
-    def flipped(name, bit):
-        return [(i, i ^ bit) for i in range(lax.axis_size(name))]
 
     def doubled(held, name, bit):
         return held + [lax.ppermute(x, name, flipped(name, bit)) for x in held]
@@ -145,6 +150,8 @@
     for bit in col_bits:
         first, second = doubled(first, "col", bit), doubled(second, "col", bit)
     second = doubled(second, "h", 1)
+    second, own_parts[1:] = lax.optimization_barrier((second, own_parts[1:]))
+    other_parts += [lax.ppermute(x, "h", flipped("h", 1)) for x in own_parts[1:]]
     pieces = doubled(first, "col", 1) + doubled(second, "col", 1)
 
     digits = jnp.stack([x[:, chunk : chunk + 3 * lines] for x in pieces])
@@ -153,20 +160,24 @@
     to_sensor, to_panel = key % group_sensors, key // group_sensors
     to_owner, to_window = to_panel // windows, to_panel % windows
     to_ring = (to_owner // halves - my_ring + ring) % ring
-    panel = (to_ring * halves + to_owner % halves) * windows + to_window
-    panels = halves * windows
+    place = (to_sensor // sensors + my_half) % halves * sensors + to_sensor % sensors
     index = jnp.where(
-        to_sensor // sensors == my_half,
-        panel * sensors + to_sensor % sensors,
-        ring * panels * sensors,
+        to_owner % halves == my_half,
+        (to_ring * windows + to_window) * group_sensors + place,
+        ring * windows * group_sensors,
     )
-    aligned = scatter_blocks(index, pieces, ring, panels, sensors)
-
-    def partial(distance):
+    aligned = scatter_blocks(index, pieces, ring, windows, group_sensors)
+
+    def full(part):
+        return jnp.concatenate([own_parts[part], other_parts[part]], axis=0)
+
+    whole = [full(part) for part in range(CHUNKS)]
+
+    def partial(distance, part):
         return lax.optimization_barrier(
             lax.dot_general(
                 aligned[distance % ring],
-                calibration,
+                whole[part],
                 (((0,), (0,)), ((), ())),
                 preferred_element_type=jnp.float32,
             ).astype(jnp.bfloat16)
@@ -175,27 +186,32 @@
     def add(a, b):
         return (a.astype(jnp.float32) + b.astype(jnp.float32)).astype(jnp.bfloat16)
 
-    ahead = [(i, (i + 1) % ring) for i in range(ring)]
-    back = [(i, (i - 1) % ring) for i in range(ring)]
-    split = outputs // 2
-    far = partial(ring // 2)
-    up = [lax.ppermute(far[:, :split], "g", ahead)]
-    down = [lax.ppermute(far[:, split:], "g", back)]
-    for distance in range(ring // 2 - 1, 0, -1):
-        rise, fall = partial(distance), partial(-distance)
-        rise_parts, fall_parts = [rise[:, :split], rise[:, split:]], [fall[:, split:], fall[:, :split]]
-        up = [lax.ppermute(add(rise_parts[i], up[i]) if i < len(up) else rise_parts[i], "g", ahead) for i in range(2)]
-        down = [lax.ppermute(add(fall_parts[i], down[i]) if i < len(down) else fall_parts[i], "g", back) for i in range(2)]
-    here = partial(0)
-    total = (
-        here.astype(jnp.float32)
-        + jnp.concatenate(up, axis=1).astype(jnp.float32)
-        + jnp.concatenate(down[::-1], axis=1).astype(jnp.float32)
-    )
-    total = total.astype(jnp.bfloat16).reshape(halves, ROWS_DEV, outputs)
-    mine = lax.dynamic_index_in_dim(total, my_half, 0, keepdims=False)
-    other = lax.dynamic_index_in_dim(total, 1 - my_half, 0, keepdims=False)
-    return add(mine, lax.ppermute(other, "h", flipped("h", 1)))
+    partials = {}
+    for distance in list(range(ring - 1, 0, -1)) + [0]:
+        for part in range(CHUNKS):
+            for sign in (1, -1):
+                at = (sign * distance % ring, part)
+                if at not in partials:
+                    partials[at] = partial(*at)
+    right, left = [None] * CHUNKS, [None] * CHUNKS
+    for distance in range(ring - 1, 0, -1):
+        ahead = [(i, i + 1) for i in range(ring - distance)]
+        back = [(i, i - 1) for i in range(distance, ring)]
+        for part in range(CHUNKS):
+            rise, fall = partials[distance, part], partials[-distance % ring, part]
+            if right[part] is not None:
+                rise, fall = add(rise, right[part]), add(fall, left[part])
+            right[part] = lax.ppermute(rise, "g", ahead)
+            left[part] = lax.ppermute(fall, "g", back)
+    total = [
+        (
+            partials[0, part].astype(jnp.float32)
+            + right[part].astype(jnp.float32)
+            + left[part].astype(jnp.float32)
+        ).astype(jnp.bfloat16)
+        for part in range(CHUNKS)
+    ]
+    return jnp.concatenate(total, axis=1)
 
 
 def solution(mesh):

time: 307 us -> 261 us (0.85)
  waiting for transfers between devices: 166 us -> 87.1 us
  starting transfers between devices: 18.4 us -> 47.2 us
  local copies, waits for them, and re-layouts: 2.14 us -> 8.87 us
  Pallas kernels: 51.7 us -> 46.6 us
  matrix products: 24.9 us -> 29.1 us
    ppermute x7 -> x14, waiting for transfers between devices: 141 us -> 32.7 us  [the longest x6 31.3 us: per_device(): right[part] = lax.ppermute(rise, 'g', ahead)]
    ppermute x7 -> x14, starting transfers between devices: 10.7 us -> 39.8 us  [the longest x6 32.3 us: per_device(): right[part] = lax.ppermute(rise, 'g', ahead)]
    ppermute x14, waiting for transfers between devices: 25.3 us -> 54.5 us  [doubled(): return held + [lax.ppermute(x, name, flipped(name, bit)) for x in held]]
    pallas_call x1, Pallas kernels: 47.5 us -> 42.4 us  [scatter_blocks(): pl.pallas_call(functools.partial(scatter_kernel, len(pieces)), grid=(owne...]
    dot_general x4 -> x8, matrix products: 24.9 us -> 29.1 us  [partial(): lax.dot_general(aligned[distance % ring], whole[part], (((0,), (0,)), (()...]
    slice x3 -> x1, local copies, waits for them, and re-layouts: 0.37 us -> 3.83 us  [per_device(): calibration[:, i * split:(i + 1) * split]]
  transfers between devices with their start and end apart: 21 -> 28, of which waited for: 12 -> 11; matrix products, arithmetic and copies ran while one was open for 4% -> 15% of each run, Pallas kernels for 0% -> 16%
where the time goes in v2:
time: 261 us; the launch traced here: 260 us
  waiting for transfers between devices  87.1 us (33%)
  starting transfers between devices  47.2 us (18%)
  Pallas kernels  46.6 us (18%)
  blocking collectives  33.6 us (13%)
  matrix products  29.1 us (11%)
  local copies, waits for them, and re-layouts  8.87 us (3%)
  other arithmetic  6.36 us (2%)
    ppermute x14, waiting for transfers between devices, doubled(): return held + [lax.ppermute(x, name, flipped(name, bit)) for x in held]  54.5 us
    pallas_call x1, Pallas kernels, scatter_blocks(): pl.pallas_call(functools.partial(scatter_kernel, len(pieces)), grid=(owne...  42.4 us
    ppermute x6, starting transfers between devices, per_device(): right[part] = lax.ppermute(rise, 'g', ahead)  32.3 us
    ppermute x6, waiting for transfers between devices, per_device(): right[part] = lax.ppermute(rise, 'g', ahead)  31.3 us
    dot_general x8, matrix products, partial(): lax.dot_general(aligned[distance % ring], whole[part], (((0,), (0,)), (()...  29.1 us
    all_to_all x1, blocking collectives, per_device(): lax.all_to_all(routed, 'g', split_axis=0, concat_axis=0, tiled=True)  20.4 us
    all_to_all x1, blocking collectives, per_device(): lax.all_to_all(routed, 'col', split_axis=0, concat_axis=0, tiled=True)  13.2 us
    ppermute x14, starting transfers between devices, doubled(): return held + [lax.ppermute(x, name, flipped(name, bit)) for x in held]  7.44 us
  transfers between devices with their start and end apart: 28, of which 11 were waited for; matrix products, arithmetic and copies ran while one was open for 15% of the time, Pallas kernels for 16%

profile of v2, /device:TPU:0, one launch (start us, length us, event | category | flops | bytes accessed | tf_op | source)
XLA Modules:
  0.0 260.0 jit_solution(7714566842354468847)
XLA Ops:
  0.7 0.7 broadcast_multiply_fusion
  1.4 0.7 and_convert_fusion.1
  2.1 0.6 pad.4.digits_ref
  2.7 1.3 add_convert_fusion.6.keys_ref
  4.1 4.2 %spread.1 = bf16[4,528,128]{2,1,0:T(8,128)(2,1)} custom-call(s32[1,1]{1,0:T(1,128)S(6)} %copy.54.count_ref, bf16[2048,128]{1,0:T(8,128)(2,1)} %bitcast.104, bf16[2048,128]{1,0:T(8,128)(2,1)} %bitcast.105, f32[4,4,128]{2,1,0:T(4,128)} %add_convert_fusion.6.keys_ref, bf16[4,16,128]{2,1,0:T(8,128)(2,1)} %pad.4.digits_ref), custom_call_target="tpu_custom_call" | custom-call | tf_op jit(solution)/shard_map/spread/pallas_call | solution.py:51
  8.3 13.2 %all_to_all.10 = bf16[4,528,128]{2,1,0:T(8,128)(2,1)S(1)} all-to-all(bf16[4,528,128]{2,1,0:T(8,128)(2,1)} %spread.1), channel_id=1, replica_groups=mesh['g'=4,'h'=2,'col'=4] {'col'}, dimensions={0} | all-to-all | bytes 1081344 | tf_op jit(solution)/shard_map/all_to_all | solution.py:141
  21.5 20.4 %all_to_all.11 = bf16[4,528,128]{2,1,0:T(8,128)(2,1)S(1)} all-to-all(bf16[4,528,128]{2,1,0:T(8,128)(2,1)S(1)} %all_to_all.10), channel_id=1, replica_groups=mesh['g'=4,'h'=2,'col'=4] {'g'}, dimensions={0} | all-to-all | bytes 1081344 | tf_op jit(solution)/shard_map/all_to_all | solution.py:142
  41.9 0.5 collective-permute-start.7
  42.4 1.5 collective-permute-start
  43.9 3.8 %fusion.41 = (bf16[2048,512]{1,0:T(8,128)(2,1)}, bf16[2048,512]{1,0:T(8,128)(2,1)S(1)}) fusion(bf16[2048,1024]{1,0:T(8,128)(2,1)} %param.13), kind=kLoop, calls=%fused_computation.128 | loop fusion | bytes 8388608 | tf_op jit(solution)/shard_map/slice | solution.py:136
  47.7 0.5 collective-permute-start.14
  48.2 1.5 collective-permute-start.8
  49.8 1.6 collective-permute-start.1
  51.4 0.5 collective-permute-start.9
  51.9 0.4 collective-permute-start.2
  52.3 0.7 constant_dynamic-update-slice_fusion.14
  53.0 6.0 %collective-permute-done.1.refs_2_ = bf16[2,528,128]{2,1,0:T(8,128)(2,1)S(1)} collective-permute-done((bf16[2,528,128]{2,1,0:T(8,128)(2,1)S(1)}, bf16[2,528,128]{2,1,0:T(8,128)(2,1)S(1)}, u32[]{:S(2)}, u32[]{:S(2)}) %collective-permute-start.1) | collective-permute-done | bytes 270368 | tf_op jit(solution)/shard_map/ppermute | solution.py:145
  59.1 43.2 %collective-permute-done.8.refs_10_ = bf16[2,528,128]{2,1,0:T(8,128)(2,1)S(1)} collective-permute-done((bf16[2,528,128]{2,1,0:T(8,128)(2,1)S(1)}, bf16[2,528,128]{2,1,0:T(8,128)(2,1)S(1)}, u32[]{:S(2)}, u32[]{:S(2)}) %collective-permute-start.8) | collective-permute-done | bytes 270368 | tf_op jit(solution)/shard_map/ppermute | solution.py:145
  102.2 3.9 %collective-permute-done.9.refs_11_ = bf16[2,528,128]{2,1,0:T(8,128)(2,1)S(1)} collective-permute-done((bf16[2,528,128]{2,1,0:T(8,128)(2,1)S(1)}, bf16[2,528,128]{2,1,0:T(8,128)(2,1)S(1)}, u32[]{:S(2)}, u32[]{:S(2)}) %collective-permute-start.9) | collective-permute-done | bytes 270368 | tf_op jit(solution)/shard_map/ppermute | solution.py:145
  106.1 0.5 collective-permute-start.10
  106.7 0.1 collective-permute-start.11
  106.8 0.5 collective-permute-start.6
  107.3 0.4 collective-permute-done.5.refs_6_
  107.8 1.0 collective-permute-done.6.refs_7_
  109.0 1.6 collective-permute-start.21
  110.7 0.8 copy-done.14
  111.5 0.7 copy-done.15
  112.4 0.9 fusion.28.index_ref
  113.4 42.4 %scatter.1 = bf16[4,4096,512]{2,1,0:T(8,128)(2,1)} custom-call(s32[16384]{0:T(1024)} %fusion.28.index_ref, bf16[2,528,128]{2,1,0:T(8,128)(2,1)} %copy-done.2, bf16[2,528,128]{2,1,0:T(8,128)(2,1)} %collective-permute-done.refs_1_, bf16[2,528,128]{2,1,0:T(8,128)(2,1)} %copy-done.5, bf16[2,528,128]{2,1,0:T(8,128)(2,1)} %copy-done.7, ...), custom_call_target="tpu_custom_call" | custom-call | tf_op jit(solution)/shard_map/scatter/pallas_call | solution.py:109
  155.8 6.0 %fusion.8 = bf16[512,512]{1,0:T(8,128)(2,1)S(1)} fusion(bf16[4,4096,512]{2,1,0:T(8,128)(2,1)} %scatter.1, bf16[2048,512]{1,0:T(8,128)(2,1)} %collective-permute-done.14, bf16[2048,512]{1,0:T(8,128)(2,1)} %get-tuple-element.17), kind=kOutput, calls=%fused_computation.17 | convolution fusion | flops 2156134400 | bytes 8912896 | tf_op jit(solution)/shard_map/dot_general | solution.py:178
  161.8 2.5 collective-permute-start.15
  164.3 4.6 %fusion.12 = bf16[512,512]{1,0:T(8,128)(2,1)S(1)} fusion(bf16[4,4096,512]{2,1,0:T(8,128)(2,1)S(1)} %copy-done, bf16[2048,512]{1,0:T(8,128)(2,1)} %collective-permute-done.14, bf16[2048,512]{1,0:T(8,128)(2,1)} %get-tuple-element.17), kind=kOutput, calls=%fused_computation.21 | convolution fusion | flops 2156134400 | bytes 8912896 | tf_op jit(solution)/shard_map/dot_general | solution.py:178
  168.9 0.7 collective-permute-start.18
  169.6 4.6 %fusion.10 = bf16[512,512]{1,0:T(8,128)(2,1)S(1)} fusion(bf16[4,4096,512]{2,1,0:T(8,128)(2,1)S(1)} %copy-done, bf16[2048,512]{1,0:T(8,128)(2,1)} %collective-permute-done.14, bf16[2048,512]{1,0:T(8,128)(2,1)} %get-tuple-element.17), kind=kOutput, calls=%fused_computation.19 | convolution fusion | flops 2156134400 | bytes 8912896 | tf_op jit(solution)/shard_map/dot_general | solution.py:178
  174.2 1.5 collective-permute-done.15
  175.7 0.3 fusion.16
  176.0 0.7 collective-permute-start.19
  176.7 5.0 %collective-permute-start.16 = (bf16[512,512]{1,0:T(8,128)(2,1)S(1)}, bf16[512,512]{1,0:T(8,128)(2,1)S(1)}, u32[]{:S(2)}, u32[]{:S(2)}) collective-permute-start(bf16[512,512]{1,0:T(8,128)(2,1)S(1)} %get-tuple-element.21), channel_id=1, source_target_pairs={{0,8},{8,16},{1,9},{9,17},{2,10},{10,18},{3,11},{11,19},{4,12},{12... | collective-permute-start | bytes 1572872 | tf_op jit(solution)/shard_map/ppermute | solution.py:204
  181.8 0.1 add_convert_fusion.4
  182.0 1.3 collective-permute-start.20
  183.3 8.9 %collective-permute-done.16 = bf16[512,512]{1,0:T(8,128)(2,1)S(1)} collective-permute-done((bf16[512,512]{1,0:T(8,128)(2,1)S(1)}, bf16[512,512]{1,0:T(8,128)(2,1)S(1)}, u32[]{:S(2)}, u32[]{:S(2)}) %collective-permute-start.16) | collective-permute-done | bytes 524320 | tf_op jit(solution)/shard_map/ppermute | solution.py:204
  192.2 0.1 add_convert_fusion.5
  192.4 11.5 %collective-permute-start.17 = (bf16[512,512]{1,0:T(8,128)(2,1)S(1)}, bf16[512,512]{1,0:T(8,128)(2,1)S(1)}, u32[]{:S(2)}, u32[]{:S(2)}) collective-permute-start(bf16[512,512]{1,0:T(8,128)(2,1)S(1)} %add_convert_fusion.5), channel_id=1, source_target_pairs={{0,8},{8,16},{16,24},{1,9},{9,17},{17,25},{2,10},{10,18},{18,26},{... | collective-permute-start | bytes 1572872 | tf_op jit(solution)/shard_map/ppermute | solution.py:204
  203.8 1.7 constant_dynamic-update-slice_fusion.16
  205.6 2.3 fusion.9
  207.9 2.3 fusion.13
  210.3 3.9 %collective-permute-start.22 = (bf16[512,512]{1,0:T(8,128)(2,1)S(1)}, bf16[512,512]{1,0:T(8,128)(2,1)S(1)}, u32[]{:S(2)}, u32[]{:S(2)}) collective-permute-start(bf16[512,512]{1,0:T(8,128)(2,1)S(1)} %fusion.9), channel_id=1, source_target_pairs={{0,8},{1,9},{2,10},{3,11},{4,12},{5,13},{6,14},{7,15}} | collective-permute-start | bytes 1572872 | tf_op jit(solution)/shard_map/ppermute | solution.py:204
  214.2 0.7 collective-permute-start.25
  214.9 2.3 fusion.11
  217.3 7.6 %collective-permute-done.22 = bf16[512,512]{1,0:T(8,128)(2,1)S(1)} collective-permute-done((bf16[512,512]{1,0:T(8,128)(2,1)S(1)}, bf16[512,512]{1,0:T(8,128)(2,1)S(1)}, u32[]{:S(2)}, u32[]{:S(2)}) %collective-permute-start.22) | collective-permute-done | bytes 524320 | tf_op jit(solution)/shard_map/ppermute | solution.py:204
  224.9 0.3 fusion.18
  225.1 0.7 collective-permute-start.26
  225.8 4.6 %fusion.14 = bf16[512,512]{1,0:T(8,128)(2,1)S(1)} fusion(bf16[4,4096,512]{2,1,0:T(8,128)(2,1)S(1)} %copy-done, bf16[2048,512]{1,0:T(8,128)(2,1)} %collective-permute-done.14, bf16[2048,512]{1,0:T(8,128)(2,1)} %get-tuple-element.17), kind=kOutput, calls=%fused_computation.23 | convolution fusion | flops 2156134400 | bytes 8912896 | tf_op jit(solution)/shard_map/dot_general | solution.py:178
  230.4 5.0 %collective-permute-start.23 = (bf16[512,512]{1,0:T(8,128)(2,1)S(1)}, bf16[512,512]{1,0:T(8,128)(2,1)S(1)}, u32[]{:S(2)}, u32[]{:S(2)}) collective-permute-start(bf16[512,512]{1,0:T(8,128)(2,1)S(1)} %get-tuple-element.23), channel_id=1, source_target_pairs={{0,8},{8,16},{1,9},{9,17},{2,10},{10,18},{3,11},{11,19},{4,12},{12... | collective-permute-start | bytes 1572872 | tf_op jit(solution)/shard_map/ppermute | solution.py:204
  235.5 0.2 add_convert_fusion.3
  235.7 0.1 add_convert_fusion.1
  235.8 1.3 collective-permute-start.27
  237.1 8.1 %collective-permute-done.23 = bf16[512,512]{1,0:T(8,128)(2,1)S(1)} collective-permute-done((bf16[512,512]{1,0:T(8,128)(2,1)S(1)}, bf16[512,512]{1,0:T(8,128)(2,1)S(1)}, u32[]{:S(2)}, u32[]{:S(2)}) %collective-permute-start.23) | collective-permute-done | bytes 524320 | tf_op jit(solution)/shard_map/ppermute | solution.py:204
  245.4 4.4 %collective-permute-start.24 = (bf16[512,512]{1,0:T(8,128)(2,1)S(1)}, bf16[512,512]{1,0:T(8,128)(2,1)S(1)}, u32[]{:S(2)}, u32[]{:S(2)}) collective-permute-start(bf16[512,512]{1,0:T(8,128)(2,1)S(1)} %add_convert_fusion.2), channel_id=1, source_target_pairs={{0,8},{8,16},{16,24},{1,9},{9,17},{17,25},{2,10},{10,18},{18,26},{... | collective-permute-start | bytes 1572872 | tf_op jit(solution)/shard_map/ppermute | solution.py:204
  249.8 2.3 fusion.15
  252.1 1.4 collective-permute-done.27
  253.6 5.1 %collective-permute-done.24 = bf16[512,512]{1,0:T(8,128)(2,1)S(1)} collective-permute-done((bf16[512,512]{1,0:T(8,128)(2,1)S(1)}, bf16[512,512]{1,0:T(8,128)(2,1)S(1)}, u32[]{:S(2)}, u32[]{:S(2)}) %collective-permute-start.24) | collective-permute-done | bytes 524320 | tf_op jit(solution)/shard_map/ppermute | solution.py:204
  258.7 0.2 add_convert_fusion
  258.9 1.1 pad_maximum_fusion.1
  (77 shorter events, 1.0 us)
Async XLA Ops:
  41.9 17.1 %copy-start.2 = (bf16[2,528,128]{2,1,0:T(8,128)(2,1)}, bf16[2,528,128]{2,1,0:T(8,128)(2,1)S(1)}, u32[]{:S(2)}) copy-start(bf16[2,528,128]{2,1,0:T(8,128)(2,1)S(1)} %get-tuple-element.19.refs_0_) | copy-start | bytes 811012
  41.9 67.1 %copy-start.1 = (bf16[2,528,128]{2,1,0:T(8,128)(2,1)}, bf16[2,528,128]{2,1,0:T(8,128)(2,1)S(1)}, u32[]{:S(2)}) copy-start(bf16[2,528,128]{2,1,0:T(8,128)(2,1)S(1)} %get-tuple-element.10.refs_8_) | copy-start | bytes 811012
  41.9 9.5 %collective-permute-start.7 = (bf16[2,528,128]{2,1,0:T(8,128)(2,1)S(1)}, bf16[2,528,128]{2,1,0:T(8,128)(2,1)S(1)}, u32[]{:S(2)}, u32[]{:S(2)}) collective-permute-start(bf16[2,528,128]{2,1,0:T(8,128)(2,1)S(1)} %get-tuple-element.10.refs_8_), channel_id=1, source_target_pairs={{0,2},{1,3},{2,0},{3,1},{4,6},{5,7},{6,4},{7,5},{8,10},{9,11},{10,... | collective-permute-start | bytes 811016 | tf_op jit(solution)/shard_map/ppermute | solution.py:145
  42.4 9.5 %collective-permute-start = (bf16[2,528,128]{2,1,0:T(8,128)(2,1)S(1)}, bf16[2,528,128]{2,1,0:T(8,128)(2,1)}, u32[]{:S(2)}, u32[]{:S(2)}) collective-permute-start(bf16[2,528,128]{2,1,0:T(8,128)(2,1)S(1)} %get-tuple-element.19.refs_0_), channel_id=1, source_target_pairs={{0,4},{4,0},{1,5},{5,1},{2,6},{6,2},{3,7},{7,3},{8,12},{12,8},{9,1... | collective-permute-start | bytes 811016 | tf_op jit(solution)/shard_map/ppermute | solution.py:145
  47.7 108.1 %collective-permute-start.14 = (bf16[2048,512]{1,0:T(8,128)(2,1)}, bf16[2048,512]{1,0:T(8,128)(2,1)}, u32[]{:S(2)}, u32[]{:S(2)}) collective-permute-start(bf16[2048,512]{1,0:T(8,128)(2,1)} %get-tuple-element.17), channel_id=1, source_target_pairs={{0,4},{4,0},{1,5},{5,1},{2,6},{6,2},{3,7},{7,3},{8,12},{12,8},{9,1... | collective-permute-start | bytes 6291464 | tf_op jit(solution)/shard_map/ppermute | solution.py:137
  48.2 54.0 %collective-permute-start.8 = (bf16[2,528,128]{2,1,0:T(8,128)(2,1)S(1)}, bf16[2,528,128]{2,1,0:T(8,128)(2,1)S(1)}, u32[]{:S(2)}, u32[]{:S(2)}) collective-permute-start(bf16[2,528,128]{2,1,0:T(8,128)(2,1)S(1)} %get-tuple-element.10.refs_8_), channel_id=1, source_target_pairs={{0,4},{4,0},{1,5},{5,1},{2,6},{6,2},{3,7},{7,3},{8,12},{12,8},{9,1... | collective-permute-start | bytes 811016 | tf_op jit(solution)/shard_map/ppermute | solution.py:145
  49.8 9.3 %collective-permute-start.1 = (bf16[2,528,128]{2,1,0:T(8,128)(2,1)S(1)}, bf16[2,528,128]{2,1,0:T(8,128)(2,1)S(1)}, u32[]{:S(2)}, u32[]{:S(2)}) collective-permute-start(bf16[2,528,128]{2,1,0:T(8,128)(2,1)S(1)} %get-tuple-element.19.refs_0_), channel_id=1, source_target_pairs={{0,2},{1,3},{2,0},{3,1},{4,6},{5,7},{6,4},{7,5},{8,10},{9,11},{10,... | collective-permute-start | bytes 811016 | tf_op jit(solution)/shard_map/ppermute | solution.py:145
  51.4 62.0 %copy-start.3 = (bf16[2,528,128]{2,1,0:T(8,128)(2,1)}, bf16[2,528,128]{2,1,0:T(8,128)(2,1)S(1)}, u32[]{:S(2)}) copy-start(bf16[2,528,128]{2,1,0:T(8,128)(2,1)S(1)} %collective-permute-done.7.refs_9_) | copy-start | bytes 811012
  51.4 54.7 %collective-permute-start.9 = (bf16[2,528,128]{2,1,0:T(8,128)(2,1)S(1)}, bf16[2,528,128]{2,1,0:T(8,128)(2,1)S(1)}, u32[]{:S(2)}, u32[]{:S(2)}) collective-permute-start(bf16[2,528,128]{2,1,0:T(8,128)(2,1)S(1)} %collective-permute-done.7.refs_9_), channel_id=1, source_target_pairs={{0,4},{4,0},{1,5},{5,1},{2,6},{6,2},{3,7},{7,3},{8,12},{12,8},{9,1... | collective-permute-start | bytes 811016 | tf_op jit(solution)/shard_map/ppermute | solution.py:145
  51.9 54.2 %collective-permute-start.2 = (bf16[2,528,128]{2,1,0:T(8,128)(2,1)}, bf16[2,528,128]{2,1,0:T(8,128)(2,1)S(1)}, u32[]{:S(2)}, u32[]{:S(2)}) collective-permute-start(bf16[2,528,128]{2,1,0:T(8,128)(2,1)} %collective-permute-done.refs_1_), channel_id=1, source_target_pairs={{0,2},{1,3},{2,0},{3,1},{4,6},{5,7},{6,4},{7,5},{8,10},{9,11},{10,... | collective-permute-start | bytes 811016 | tf_op jit(solution)/shard_map/ppermute | solution.py:145
  59.0 54.3 %copy-start.5 = (bf16[2,528,128]{2,1,0:T(8,128)(2,1)}, bf16[2,528,128]{2,1,0:T(8,128)(2,1)S(1)}, u32[]{:S(2)}) copy-start(bf16[2,528,128]{2,1,0:T(8,128)(2,1)S(1)} %collective-permute-done.1.refs_2_) | copy-start | bytes 811012
  59.0 47.6 %collective-permute-start.3 = (bf16[2,528,128]{2,1,0:T(8,128)(2,1)S(1)}, bf16[2,528,128]{2,1,0:T(8,128)(2,1)S(1)}, u32[]{:S(2)}, u32[]{:S(2)}) collective-permute-start(bf16[2,528,128]{2,1,0:T(8,128)(2,1)S(1)} %get-tuple-element.19.refs_0_), channel_id=1, source_target_pairs={{0,1},{1,0},{2,3},{3,2},{4,5},{5,4},{6,7},{7,6},{8,9},{9,8},{10,11... | collective-permute-start | bytes 811016 | tf_op jit(solution)/shard_map/ppermute | solution.py:145
  102.2 11.1 %copy-start.4 = (bf16[2,528,128]{2,1,0:T(8,128)(2,1)}, bf16[2,528,128]{2,1,0:T(8,128)(2,1)S(1)}, u32[]{:S(2)}) copy-start(bf16[2,528,128]{2,1,0:T(8,128)(2,1)S(1)} %collective-permute-done.8.refs_10_) | copy-start | bytes 811012
  102.2 4.6 %collective-permute-start.4 = (bf16[2,528,128]{2,1,0:T(8,128)(2,1)}, bf16[2,528,128]{2,1,0:T(8,128)(2,1)S(1)}, u32[]{:S(2)}, u32[]{:S(2)}) collective-permute-start(bf16[2,528,128]{2,1,0:T(8,128)(2,1)} %collective-permute-done.refs_1_), channel_id=1, source_target_pairs={{0,1},{1,0},{2,3},{3,2},{4,5},{5,4},{6,7},{7,6},{8,9},{9,8},{10,11... | collective-permute-start | bytes 811016 | tf_op jit(solution)/shard_map/ppermute | solution.py:145
  106.1 7.2 %copy-start.6 = (bf16[2,528,128]{2,1,0:T(8,128)(2,1)}, bf16[2,528,128]{2,1,0:T(8,128)(2,1)S(1)}, u32[]{:S(2)}) copy-start(bf16[2,528,128]{2,1,0:T(8,128)(2,1)S(1)} %collective-permute-done.9.refs_11_) | copy-start | bytes 811012
  106.1 1.5 collective-permute-start.5
  106.1 7.2 %copy-start.7 = (bf16[2,528,128]{2,1,0:T(8,128)(2,1)}, bf16[2,528,128]{2,1,0:T(8,128)(2,1)S(1)}, u32[]{:S(2)}) copy-start(bf16[2,528,128]{2,1,0:T(8,128)(2,1)S(1)} %collective-permute-done.2.refs_3_) | copy-start | bytes 811012
  106.1 2.9 %collective-permute-start.10 = (bf16[2,528,128]{2,1,0:T(8,128)(2,1)S(1)}, bf16[2,528,128]{2,1,0:T(8,128)(2,1)S(1)}, u32[]{:S(2)}, u32[]{:S(2)}) collective-permute-start(bf16[2,528,128]{2,1,0:T(8,128)(2,1)S(1)} %get-tuple-element.10.refs_8_), channel_id=1, source_target_pairs={{0,1},{1,0},{2,3},{3,2},{4,5},{5,4},{6,7},{7,6},{8,9},{9,8},{10,11... | collective-permute-start | bytes 811016 | tf_op jit(solution)/shard_map/ppermute | solution.py:145
  106.7 5.5 %copy-start.8 = (bf16[2,528,128]{2,1,0:T(8,128)(2,1)}, bf16[2,528,128]{2,1,0:T(8,128)(2,1)S(1)}, u32[]{:S(2)}) copy-start(bf16[2,528,128]{2,1,0:T(8,128)(2,1)S(1)} %collective-permute-done.3.refs_4_) | copy-start | bytes 811012
  106.7 4.0 %collective-permute-start.11 = (bf16[2,528,128]{2,1,0:T(8,128)(2,1)S(1)}, bf16[2,528,128]{2,1,0:T(8,128)(2,1)S(1)}, u32[]{:S(2)}, u32[]{:S(2)}) collective-permute-start(bf16[2,528,128]{2,1,0:T(8,128)(2,1)S(1)} %collective-permute-done.7.refs_9_), channel_id=1, source_target_pairs={{0,1},{1,0},{2,3},{3,2},{4,5},{5,4},{6,7},{7,6},{8,9},{9,8},{10,11... | collective-permute-start | bytes 811016 | tf_op jit(solution)/shard_map/ppermute | solution.py:145
  106.8 5.4 %copy-start.9 = (bf16[2,528,128]{2,1,0:T(8,128)(2,1)}, bf16[2,528,128]{2,1,0:T(8,128)(2,1)S(1)}, u32[]{:S(2)}) copy-start(bf16[2,528,128]{2,1,0:T(8,128)(2,1)S(1)} %collective-permute-done.4.refs_5_) | copy-start | bytes 811012
  106.8 2.0 collective-permute-start.6
  107.7 4.5 %copy-start.10 = (bf16[2,528,128]{2,1,0:T(8,128)(2,1)}, bf16[2,528,128]{2,1,0:T(8,128)(2,1)S(1)}, u32[]{:S(2)}) copy-start(bf16[2,528,128]{2,1,0:T(8,128)(2,1)S(1)} %collective-permute-done.5.refs_6_) | copy-start | bytes 811012
  107.7 3.0 %collective-permute-start.12 = (bf16[2,528,128]{2,1,0:T(8,128)(2,1)S(1)}, bf16[2,528,128]{2,1,0:T(8,128)(2,1)S(1)}, u32[]{:S(2)}, u32[]{:S(2)}) collective-permute-start(bf16[2,528,128]{2,1,0:T(8,128)(2,1)S(1)} %collective-permute-done.8.refs_10_), channel_id=1, source_target_pairs={{0,1},{1,0},{2,3},{3,2},{4,5},{5,4},{6,7},{7,6},{8,9},{9,8},{10,11... | collective-permute-start | bytes 811016 | tf_op jit(solution)/shard_map/ppermute | solution.py:145
  108.8 3.4 %copy-start.13 = (bf16[2,528,128]{2,1,0:T(8,128)(2,1)}, bf16[2,528,128]{2,1,0:T(8,128)(2,1)S(1)}, u32[]{:S(2)}) copy-start(bf16[2,528,128]{2,1,0:T(8,128)(2,1)S(1)} %collective-permute-done.6.refs_7_) | copy-start | bytes 811012
  108.8 1.8 collective-permute-start.13
  109.0 3.2 %copy-start.11 = (bf16[2,528,128]{2,1,0:T(8,128)(2,1)}, bf16[2,528,128]{2,1,0:T(8,128)(2,1)S(1)}, u32[]{:S(2)}) copy-start(bf16[2,528,128]{2,1,0:T(8,128)(2,1)S(1)} %collective-permute-done.10.refs_12_) | copy-start | bytes 811012
  109.0 94.8 %collective-permute-start.21 = (bf16[2048,512]{1,0:T(8,128)(2,1)S(1)}, bf16[2048,512]{1,0:T(8,128)(2,1)}, u32[]{:S(2)}, u32[]{:S(2)}) collective-permute-start(bf16[2048,512]{1,0:T(8,128)(2,1)S(1)} %get-tuple-element.14), channel_id=1, source_target_pairs={{0,4},{4,0},{1,5},{5,1},{2,6},{6,2},{3,7},{7,3},{8,12},{12,8},{9,1... | collective-permute-start | bytes 6291464 | tf_op jit(solution)/shard_map/ppermute | solution.py:154
  110.6 2.7 %copy-start.12 = (bf16[2,528,128]{2,1,0:T(8,128)(2,1)}, bf16[2,528,128]{2,1,0:T(8,128)(2,1)S(1)}, u32[]{:S(2)}) copy-start(bf16[2,528,128]{2,1,0:T(8,128)(2,1)S(1)} %collective-permute-done.11.refs_13_) | copy-start | bytes 811012
  110.7 0.8 copy-start.14
  111.5 0.7 copy-start.15
  155.8 8.5 %copy-start = (bf16[4,4096,512]{2,1,0:T(8,128)(2,1)S(1)}, bf16[4,4096,512]{2,1,0:T(8,128)(2,1)}, u32[]{:S(2)}) copy-start(bf16[4,4096,512]{2,1,0:T(8,128)(2,1)} %scatter.1) | copy-start | bytes 50331652
  161.8 13.9 %collective-permute-start.15 = (bf16[512,512]{1,0:T(8,128)(2,1)S(1)}, bf16[512,512]{1,0:T(8,128)(2,1)S(1)}, u32[]{:S(2)}, u32[]{:S(2)}) collective-permute-start(bf16[512,512]{1,0:T(8,128)(2,1)S(1)} %fusion.8), channel_id=1, source_target_pairs={{0,8},{1,9},{2,10},{3,11},{4,12},{5,13},{6,14},{7,15}} | collective-permute-start | bytes 1572872 | tf_op jit(solution)/shard_map/ppermute | solution.py:204
  168.9 6.8 %collective-permute-start.18 = (bf16[512,512]{1,0:T(8,128)(2,1)S(1)}, bf16[512,512]{1,0:T(8,128)(2,1)S(1)}, u32[]{:S(2)}, u32[]{:S(2)}) collective-permute-start(bf16[512,512]{1,0:T(8,128)(2,1)S(1)} %fusion.12), channel_id=1, source_target_pairs={{24,16},{25,17},{26,18},{27,19},{28,20},{29,21},{30,22},{31,23}} | collective-permute-start | bytes 1572872 | tf_op jit(solution)/shard_map/ppermute | solution.py:205
  176.0 5.9 %collective-permute-start.19 = (bf16[512,512]{1,0:T(8,128)(2,1)S(1)}, bf16[512,512]{1,0:T(8,128)(2,1)S(1)}, u32[]{:S(2)}, u32[]{:S(2)}) collective-permute-start(bf16[512,512]{1,0:T(8,128)(2,1)S(1)} %get-tuple-element.22), channel_id=1, source_target_pairs={{16,8},{24,16},{17,9},{25,17},{18,10},{26,18},{19,11},{27,19},{20,... | collective-permute-start | bytes 1572872 | tf_op jit(solution)/shard_map/ppermute | solution.py:205
  176.7 15.6 %collective-permute-start.16 = (bf16[512,512]{1,0:T(8,128)(2,1)S(1)}, bf16[512,512]{1,0:T(8,128)(2,1)S(1)}, u32[]{:S(2)}, u32[]{:S(2)}) collective-permute-start(bf16[512,512]{1,0:T(8,128)(2,1)S(1)} %get-tuple-element.21), channel_id=1, source_target_pairs={{0,8},{8,16},{1,9},{9,17},{2,10},{10,18},{3,11},{11,19},{4,12},{12... | collective-permute-start | bytes 1572872 | tf_op jit(solution)/shard_map/ppermute | solution.py:204
  182.0 53.5 %collective-permute-start.20 = (bf16[512,512]{1,0:T(8,128)(2,1)S(1)}, bf16[512,512]{1,0:T(8,128)(2,1)S(1)}, u32[]{:S(2)}, u32[]{:S(2)}) collective-permute-start(bf16[512,512]{1,0:T(8,128)(2,1)S(1)} %add_convert_fusion.4), channel_id=1, source_target_pairs={{8,0},{16,8},{24,16},{9,1},{17,9},{25,17},{10,2},{18,10},{26,18},{... | collective-permute-start | bytes 1572872 | tf_op jit(solution)/shard_map/ppermute | solution.py:205
  192.4 43.1 %collective-permute-start.17 = (bf16[512,512]{1,0:T(8,128)(2,1)S(1)}, bf16[512,512]{1,0:T(8,128)(2,1)S(1)}, u32[]{:S(2)}, u32[]{:S(2)}) collective-permute-start(bf16[512,512]{1,0:T(8,128)(2,1)S(1)} %add_convert_fusion.5), channel_id=1, source_target_pairs={{0,8},{8,16},{16,24},{1,9},{9,17},{17,25},{2,10},{10,18},{18,26},{... | collective-permute-start | bytes 1572872 | tf_op jit(solution)/shard_map/ppermute | solution.py:204
  210.3 14.6 %collective-permute-start.22 = (bf16[512,512]{1,0:T(8,128)(2,1)S(1)}, bf16[512,512]{1,0:T(8,128)(2,1)S(1)}, u32[]{:S(2)}, u32[]{:S(2)}) collective-permute-start(bf16[512,512]{1,0:T(8,128)(2,1)S(1)} %fusion.9), channel_id=1, source_target_pairs={{0,8},{1,9},{2,10},{3,11},{4,12},{5,13},{6,14},{7,15}} | collective-permute-start | bytes 1572872 | tf_op jit(solution)/shard_map/ppermute | solution.py:204
  214.2 10.6 %collective-permute-start.25 = (bf16[512,512]{1,0:T(8,128)(2,1)S(1)}, bf16[512,512]{1,0:T(8,128)(2,1)S(1)}, u32[]{:S(2)}, u32[]{:S(2)}) collective-permute-start(bf16[512,512]{1,0:T(8,128)(2,1)S(1)} %fusion.13), channel_id=1, source_target_pairs={{24,16},{25,17},{26,18},{27,19},{28,20},{29,21},{30,22},{31,23}} | collective-permute-start | bytes 1572872 | tf_op jit(solution)/shard_map/ppermute | solution.py:205
  225.1 10.6 %collective-permute-start.26 = (bf16[512,512]{1,0:T(8,128)(2,1)S(1)}, bf16[512,512]{1,0:T(8,128)(2,1)S(1)}, u32[]{:S(2)}, u32[]{:S(2)}) collective-permute-start(bf16[512,512]{1,0:T(8,128)(2,1)S(1)} %get-tuple-element.24), channel_id=1, source_target_pairs={{16,8},{24,16},{17,9},{25,17},{18,10},{26,18},{19,11},{27,19},{20,... | collective-permute-start | bytes 1572872 | tf_op jit(solution)/shard_map/ppermute | solution.py:205
  230.4 14.8 %collective-permute-start.23 = (bf16[512,512]{1,0:T(8,128)(2,1)S(1)}, bf16[512,512]{1,0:T(8,128)(2,1)S(1)}, u32[]{:S(2)}, u32[]{:S(2)}) collective-permute-start(bf16[512,512]{1,0:T(8,128)(2,1)S(1)} %get-tuple-element.23), channel_id=1, source_target_pairs={{0,8},{8,16},{1,9},{9,17},{2,10},{10,18},{3,11},{11,19},{4,12},{12... | collective-permute-start | bytes 1572872 | tf_op jit(solution)/shard_map/ppermute | solution.py:204
  235.8 17.7 %collective-permute-start.27 = (bf16[512,512]{1,0:T(8,128)(2,1)S(1)}, bf16[512,512]{1,0:T(8,128)(2,1)S(1)}, u32[]{:S(2)}, u32[]{:S(2)}) collective-permute-start(bf16[512,512]{1,0:T(8,128)(2,1)S(1)} %add_convert_fusion.1), channel_id=1, source_target_pairs={{8,0},{16,8},{24,16},{9,1},{17,9},{25,17},{10,2},{18,10},{26,18},{... | collective-permute-start | bytes 1572872 | tf_op jit(solution)/shard_map/ppermute | solution.py:205
  245.4 13.3 %collective-permute-start.24 = (bf16[512,512]{1,0:T(8,128)(2,1)S(1)}, bf16[512,512]{1,0:T(8,128)(2,1)S(1)}, u32[]{:S(2)}, u32[]{:S(2)}) collective-permute-start(bf16[512,512]{1,0:T(8,128)(2,1)S(1)} %add_convert_fusion.2), channel_id=1, source_target_pairs={{0,8},{8,16},{16,24},{1,9},{9,17},{17,25},{2,10},{10,18},{18,26},{... | collective-permute-start | bytes 1572872 | tf_op jit(solution)/shard_map/ppermute | solution.py:204
